TPU v7x, 256 devices: a whole 4x4x8 slice. The times are simulated.
256 devices in a mesh: rows: 16 (over z_lo, x), cols: 16 (over y, z_hi, core).
Axes of the slice: x: 4, y: 4, z: 8 (z_hi: 2, z_lo: 4; z = z_hi * 4 + z_lo), core: 2. Of those that a mesh axis runs over, the one named last changes fastest.
Arguments:
- kernel_hat: bfloat16 [2, 256, 512, 4096], P(None, 'rows', 'cols'), may hold values from -0.5 to 0.5
- coefficients: float32 [128, 512], P(None, 'cols'), may hold values from -6 to 6
- wave_speed_sq: float32 [4096, 4096], P('rows', 'cols'), may hold values from 1 to 4
- wet_mask: int32 [4096, 4096], P('rows', 'cols'), may hold values 0 or 1
- boundary_cell: int32 [4096], replicated, may hold values from 0 to 4095, each once
- height: float32 [4096, 4096], P('rows', 'cols'), may hold values from -3 to 3
- flux_x: float32 [4096, 4096], P('rows', 'cols'), may hold values from -3 to 3
- flux_y: float32 [4096, 4096], P('rows', 'cols'), may hold values from -3 to 3
Outputs:
- boundary_series: float32 [128, 4096], P('rows', 'cols')
- height_out: float32 [4096, 4096], P('rows', 'cols')
- flux_x_out: float32 [4096, 4096], P('rows', 'cols')
- flux_y_out: float32 [4096, 4096], P('rows', 'cols')
Inputs may be any that keep to these rules, and one draw needn't show every extreme that they name: `boundary_cell`: each of the 4096 boundary points names a different grid column, so each column is named by exactly one point.
All inputs are finite; a program needn't handle non-finite values. No bound on the sum of `wet_mask` on one device may be relied on, other than what follows from the above.
Results may differ from a plain program's by a relative error of at most 0.0029.
Values sent between devices are 32-bit elements; how exact they have to be, the bound alone decides.
A program may use at most 64 MiB of HBM per device.

v0:
```python
import functools
import math

import jax
import jax.numpy as jnp
import numpy as np
from jax import lax
from jax.experimental import pallas as pl
from jax.experimental.pallas import tpu as pltpu
from jax.sharding import PartitionSpec as P

MESH = pl.DeviceIdType.MESH
GROUP = 8
X, Y, Z_LOW, Z_HIGH, CORES = 4, 4, 4, 2, 2
Y_ORDER = (2, 1, 3, 0)
BARRIER_AFTER = 3
EDGE = 8
LANE = 128
F32 = jnp.float32
BF16 = jnp.bfloat16


def tables(freq_total, steps, row_devs):
    freq = np.arange(freq_total)
    time = np.arange(steps)
    phase = 2.0 * math.pi * (np.outer(freq, time) % freq_total) / freq_total
    cos = np.cos(phase).reshape(row_devs, -1, GROUP, steps)
    sin = np.sin(phase).reshape(row_devs, -1, GROUP, steps)
    both = np.concatenate([cos, -sin], axis=2).reshape(row_devs, -1, steps)
    forward = both.astype(np.float32)
    inverse = np.swapaxes(both, 1, 2) / freq_total
    high = inverse.astype(np.float32).astype(jnp.bfloat16)
    low = (inverse - high.astype(np.float64)).astype(np.float32).astype(jnp.bfloat16)
    return forward, np.concatenate([high, high, low], axis=2)


def split(value):
    high = value.astype(BF16)
    return high, value - high.astype(F32)


def faces(speed, wet, dim):
    ahead = speed.shape[dim] - 1
    opened = wet * pltpu.roll(wet, ahead, dim)
    return 0.5 * opened, opened * (0.25 * (speed + pltpu.roll(speed, ahead, dim)))


def step_once(surf, qx, qy, speed_sq, wet, face_x, face_y):
    energy = speed_sq * surf
    change = []
    for dim, along, across, (half, damp) in ((1, qx, qy, face_x), (0, qy, qx, face_y)):
        ahead = surf.shape[dim] - 1
        later = lambda v: pltpu.roll(v, ahead, dim)
        mass = half * (along + later(along)) - damp * (later(surf) - surf)
        momentum = half * (energy + later(energy)) - damp * (later(along) - along)
        shear = -damp * (later(across) - across)
        change.append([f - pltpu.roll(f, 1, dim) for f in (mass, momentum, shear)])
    (mass_x, mom_x, shear_x), (mass_y, mom_y, shear_y) = change
    return (
        wet * (surf - 0.25 * (mass_x + mass_y)),
        wet * (qx - 0.25 * (mom_x + shear_y)),
        wet * (qy - 0.25 * (shear_x + mom_y)),
    )


def kernel(
    n_rows, n_cols,
    kern_hbm, coef_hbm, sq_hbm, wet_hbm, cell_hbm, surf_hbm, qx_hbm, qy_hbm, fwd_hbm, inv_hbm,
    series_buf, out_buf,
    kern, coef, fwd, inv, cells, pad, wet_int, corner, strip_out, strip_in,
    part, core_in, y_out, y_in, z_out, z_in, whole_buf, whole_in,
    late_part, late_in, late_out, edge_in, last_out, last_in, latest_buf, mid, chosen_buf,
    local_sem, kern_sem, core_recv, halo_send, halo_recv, late_send, send_sem, recv_sem,
):
    row = lax.axis_index("rows")
    col = lax.axis_index("cols")
    x, z_low = lax.rem(row, X), row // X
    y, z_high, core = col // (Z_HIGH * CORES), lax.rem(col // CORES, Z_HIGH), lax.rem(col, CORES)
    z = z_high * Z_LOW + z_low
    freqs, src = kern.shape[2:4]
    groups = freqs // GROUP
    tall, wide = surf_hbm.shape
    obs = cells.shape[1]
    points = obs // n_cols
    per_y = obs // Y
    own_steps = series_buf.shape[0]
    has_n, has_s = row > 0, row < n_rows - 1
    has_w, has_e = col > 0, col < n_cols - 1
    at_edge = row == n_rows - 1

    def column(y_at, z_high_at, core_at):
        return (y_at * Z_HIGH + z_high_at) * CORES + core_at

    inputs = [
        pltpu.make_async_copy(coef_hbm, coef, local_sem.at[0]),
        pltpu.make_async_copy(fwd_hbm.at[row], fwd, local_sem.at[1]),
        pltpu.make_async_copy(inv_hbm.at[row], inv, local_sem.at[2]),
        pltpu.make_async_copy(surf_hbm, pad.at[0, :tall, :wide], local_sem.at[3]),
        pltpu.make_async_copy(qx_hbm, pad.at[1, :tall, :wide], local_sem.at[4]),
        pltpu.make_async_copy(qy_hbm, pad.at[2, :tall, :wide], local_sem.at[5]),
        pltpu.make_async_copy(sq_hbm, pad.at[3, :tall, :wide], local_sem.at[6]),
        pltpu.make_async_copy(wet_hbm, wet_int, local_sem.at[7]),
        pltpu.make_async_copy(cell_hbm, cells, local_sem.at[8]),
    ]
    for copy in inputs[:3]:
        copy.start()
    chunks = []
    for i, dy in enumerate(Y_ORDER):
        at = pl.multiple_of(lax.rem(y + dy, Y) * per_y, per_y)
        for p in range(2):
            copy = pltpu.make_async_copy(
                kern_hbm.at[p, :, :, pl.ds(at, per_y)], kern.at[i, p], kern_sem.at[i, p]
            )
            copy.start()
            chunks.append(copy)
    for copy in inputs[3:]:
        copy.start()

    diagonals = [
        (has_n & has_w, -1, -1), (has_n & has_e, -1, 1),
        (has_s & has_w, 1, -1), (has_s & has_e, 1, 1),
    ]
    plane = [(dy, dc) for dy in range(Y) for dc in range(CORES) if dy or dc]
    barrier = pltpu.get_barrier_semaphore()

    def greet(to):
        pl.semaphore_signal(barrier, 1, device_id=to, device_id_type=MESH)

    def beside_me(dy, dc):
        return (row, column(lax.rem(y + dy, Y), z_high, lax.rem(core + dc, CORES)))

    partner_z = (row, column(y, 1 - z_high, core))
    partner_core = (row, column(y, z_high, 1 - core))
    for k in range(1, n_rows):
        greet((lax.rem(row + k, n_rows), col))
    greet(partner_z)
    for dy, dc in plane:
        greet(beside_me(dy, dc))
    sides = [(has_w, 0, -1), (has_e, 0, 1)] + diagonals
    for exists, dr, dc in sides:
        @pl.when(exists)
        def _(dr=dr, dc=dc):
            greet((row + dr, col + dc))

    @pl.when(at_edge)
    def _():
        for r in range(n_rows - 1):
            greet((r, partner_z[1]))
        for k in range(1, n_cols):
            greet((row, lax.rem(col + k, n_cols)))

    def remote(source, target, send, recv, to):
        return pltpu.make_async_remote_copy(
            src_ref=source, dst_ref=target, send_sem=send, recv_sem=recv,
            device_id=to, device_id_type=MESH,
        )

    def whole_wait(ref, sem):
        return remote(ref, ref, sem, sem, partner_core)

    inputs[0].wait()
    inputs[1].wait()
    spectrum = lax.dot_general(
        fwd[...], coef[...], (((1,), (1,)), ((), ())),
        precision=lax.Precision.HIGHEST, preferred_element_type=F32,
    )
    spread = jnp.where(
        lax.rem(lax.broadcasted_iota(jnp.int32, (src, GROUP * src), 1), src)
        == lax.broadcasted_iota(jnp.int32, (src, GROUP * src), 0), 1.0, 0.0
    ).astype(BF16)
    shape = (2 * GROUP, GROUP * src)
    own_block = (
        lax.broadcasted_iota(jnp.int32, shape, 1) // src
        == lax.rem(lax.broadcasted_iota(jnp.int32, shape, 0), GROUP)
    )
    lefts = []
    for g in range(groups):
        mine = spectrum[g * 2 * GROUP:(g + 1) * 2 * GROUP]
        turned = jnp.concatenate([-mine[GROUP:], mine[:GROUP]], axis=0)
        for value in (mine, turned):
            tiled = jnp.dot(value.astype(BF16), spread, preferred_element_type=F32)
            lefts.append(jnp.where(own_block, tiled, 0.0).astype(BF16))

    def send_chunk(i):
        remote(
            part.at[i, 1 - core], core_in.at[i], send_sem.at[0], core_recv.at[i], partner_core
        ).start()
        for k, (dy, dc) in enumerate(plane):
            if dy == Y_ORDER[i]:
                remote(
                    late_part.at[i, lax.rem(core + dc, CORES)], late_in.at[k],
                    send_sem.at[1], recv_sem.at[1], beside_me(dy, dc),
                ).start()

    inputs[2].wait()
    late_rows = inv[inv.shape[0] - 2 * GROUP:]
    for i in range(Y):
        chunks[2 * i].wait()
        chunks[2 * i + 1].wait()
        totals = []
        for g in range(groups):
            total = None
            for p in range(2):
                right = kern[i, p, pl.ds(g * GROUP, GROUP)].reshape(GROUP * src, per_y)
                term = jnp.dot(lefts[2 * g + p], right, preferred_element_type=F32)
                total = term if total is None else total + term
            totals.append(total)
        total = jnp.concatenate(totals, axis=0)
        high, low = split(total)
        late = jnp.dot(
            late_rows, jnp.concatenate([high, low.astype(BF16), high], axis=0),
            preferred_element_type=F32,
        )[2 * GROUP - 2:]
        for h in range(Z_HIGH):
            for c in range(CORES):
                at = (h * CORES + c) * points
                part[i, c, h] = total[:, at:at + points]
                late_part[i, c, h] = late[:, at:at + points]
        if i == BARRIER_AFTER:
            pl.semaphore_wait(
                barrier,
                n_rows - 1 + 1 + len(plane) + jnp.where(at_edge, n_cols - 1, 1)
                + sum(exists.astype(jnp.int32) for exists, _, _ in sides),
            )
            for j in range(i + 1):
                send_chunk(j)
        elif i > BARRIER_AFTER:
            send_chunk(i)

    for copy in inputs[3:8]:
        copy.wait()
    pad[4, :tall, :wide] = wet_int[...].astype(F32)
    lane = lax.broadcasted_iota(jnp.int32, (tall, LANE), 1)
    packed = jnp.zeros((tall, LANE), F32)
    for k in range(5):
        first, last = pad[k, :tall, :LANE], pad[k, :tall, wide - LANE:wide]
        at = 2 * k
        moved = first if at == 0 else pltpu.roll(first, at, 1)
        packed = jnp.where((lane >= at) & (lane < at + 2), moved, packed)
        at = 16 + 2 * k
        packed = jnp.where(
            (lane >= at) & (lane < at + 2), pltpu.roll(last, at + 2, 1), packed
        )
    strip_out[...] = packed.T[:32]

    for i in range(Y):
        whole_wait(core_in.at[i], core_recv.at[i]).wait_recv()
        if Y_ORDER[i]:
            y_out[i] = part[i, core] + core_in[i]
            remote(
                y_out.at[i], y_in.at[i], send_sem.at[2], recv_sem.at[2],
                (row, column(lax.rem(y + Y_ORDER[i], Y), z_high, core)),
            ).start()

    north = (lax.rem(row + n_rows - 1, n_rows), col)
    south = (lax.rem(row + 1, n_rows), col)
    west = (row, lax.rem(col + n_cols - 1, n_cols))
    east = (row, lax.rem(col + 1, n_cols))
    top, bottom = pl.ds(0, EDGE), pl.ds(tall - EDGE, EDGE)
    south_halo, north_halo = pl.ds(tall, EDGE), pl.ds(tall + EDGE, EDGE)
    body = pl.ds(0, wide)

    def halo(source, target, i, to):
        return remote(source, target, halo_send.at[i], halo_recv.at[i], to)

    moves = [
        (has_n, has_s, halo(pad.at[:, top, body], pad.at[:, south_halo, body], 0, north)),
        (has_s, has_n, halo(pad.at[:, bottom, body], pad.at[:, north_halo, body], 1, south)),
        (has_w, has_e, halo(strip_out.at[pl.ds(0, 16)], strip_in.at[pl.ds(16, 16)], 2, west)),
        (has_e, has_w, halo(strip_out.at[pl.ds(16, 16)], strip_in.at[pl.ds(0, 16)], 3, east)),
    ]
    for i, (exists, dr, dc) in enumerate(diagonals):
        rows_at = top if dr < 0 else bottom
        cols_at = pl.ds(0, LANE) if dc < 0 else pl.ds(wide - LANE, LANE)
        to = (lax.rem(row + dr + n_rows, n_rows), lax.rem(col + dc + n_cols, n_cols))
        moves.append((
            exists, diagonals[3 - i][0],
            halo(pad.at[:, rows_at, cols_at], corner.at[i], 4 + i, to),
        ))
    for exists, _, copy in moves:
        @pl.when(exists)
        def _(copy=copy):
            copy.start()

    whole_wait(late_in, recv_sem.at[1]).wait_recv()
    late = late_part[Y - 1, core]
    for k in range(len(plane)):
        late = late + late_in[k]
    late_out[...] = late
    for h in range(Z_HIGH):
        @pl.when(jnp.logical_not(at_edge & (z_high == h)))
        def _(h=h):
            ahead = lax.rem(h * Z_LOW + Z_LOW - 1 - z + Z_LOW * Z_HIGH, Z_LOW * Z_HIGH)
            slot = lax.max(ahead * X + X - 1 - x - 1, 0)
            remote(
                late_out.at[h], edge_in.at[slot], late_send.at[h], recv_sem.at[3],
                (n_rows - 1, column(y, h, core)),
            ).start()

    whole_wait(y_in, recv_sem.at[2]).wait_recv()
    value = part[Y - 1, core] + core_in[Y - 1]
    for i in range(Y - 1):
        value = value + y_in[i]
    z_out[...] = value
    z_copy = remote(z_out.at[1 - z_high], z_in, send_sem.at[3], recv_sem.at[4], partner_z)
    z_copy.start()

    for i, (_, arrives, copy) in enumerate(moves):
        @pl.when(arrives)
        def _(copy=copy):
            copy.wait_recv()

        @pl.when(jnp.logical_not(arrives))
        def _(i=i):
            if i == 0:
                pad[:, south_halo, body] = jnp.zeros((5, EDGE, wide), F32)
            elif i == 1:
                pad[:, north_halo, body] = jnp.zeros((5, EDGE, wide), F32)
            elif i == 2:
                strip_in[pl.ds(16, 16)] = jnp.zeros((16, tall), F32)
            elif i == 3:
                strip_in[pl.ds(0, 16)] = jnp.zeros((16, tall), F32)
            else:
                corner[i - 4] = jnp.zeros((5, EDGE, LANE), F32)

    beside = jnp.concatenate([strip_in[...], jnp.zeros((LANE - 32, tall), F32)], axis=0).T
    near = lax.broadcasted_iota(jnp.int32, (EDGE, LANE), 1) < LANE // 2
    for k in range(5):
        pad[k, :tall, wide:] = jnp.where(
            lane < LANE // 2,
            pltpu.roll(beside, LANE - 16 - 2 * k, 1),
            pltpu.roll(beside, LANE - 2 - 2 * k, 1),
        )
        pad[k, tall:tall + EDGE, wide:] = jnp.where(near, corner[0, k], corner[1, k])
        pad[k, tall + EDGE:, wide:] = jnp.where(near, corner[2, k], corner[3, k])

    @pl.when(at_edge)
    def _():
        pad[3:5, tall:tall + 1, :] = jnp.ones((2, 1, wide + LANE), F32)

    def first_step():
        wet, speed_sq = pad[4], pad[3]
        speed = jnp.sqrt(speed_sq)
        face_x, face_y = faces(speed, wet, 1), faces(speed, wet, 0)
        new = step_once(pad[0], pad[1], pad[2], speed_sq, wet, face_x, face_y)
        for k in range(3):
            mid[k] = new[k]

    def second_step():
        wet, speed_sq = pad[4], pad[3]
        speed = jnp.sqrt(speed_sq)
        face_x, face_y = faces(speed, wet, 1), faces(speed, wet, 0)
        new = step_once(mid[0], mid[1], mid[2], speed_sq, wet, face_x, face_y)
        for k in range(3):
            out_buf[k] = new[k][:tall, :wide]

    first_step()

    whole_wait(z_in, recv_sem.at[4]).wait_recv()
    high, low = split(z_out[z_high] + z_in[...])
    whole = jnp.dot(
        inv[...], jnp.concatenate([high, low.astype(BF16), high], axis=0),
        preferred_element_type=F32,
    )
    whole_buf[...] = whole
    for k in range(1, n_rows):
        to = lax.rem(row + k, n_rows)
        remote(
            whole_buf.at[pl.ds(pl.multiple_of(to * own_steps, own_steps), own_steps)],
            whole_in.at[k - 1], send_sem.at[4], recv_sem.at[5], (to, col),
        ).start()

    inputs[8].wait()
    span = wide + LANE

    @pl.when(at_edge)
    def _():
        whole_wait(edge_in, recv_sem.at[3]).wait_recv()
        value = late_out[z_high]
        for k in range(Z_LOW * Z_HIGH * X - 1):
            value = value + edge_in[k]
        last_out[...] = value
        latest_buf[col] = value
        for k in range(1, n_cols):
            remote(
                last_out, last_in.at[k - 1], send_sem.at[5], recv_sem.at[6],
                (row, lax.rem(col + k, n_cols)),
            ).start()
        place = lax.broadcasted_iota(jnp.int32, (span, obs), 0)
        place = jnp.where(place >= wide + LANE // 2, place - span, place) + col * wide
        chosen_buf[...] = jnp.where(place == cells[...], 1.0, 0.0).astype(BF16)

    second_step()

    whole_wait(whole_in, recv_sem.at[5]).wait_recv()
    value = whole_buf[pl.ds(pl.multiple_of(row * own_steps, own_steps), own_steps)]
    for k in range(1, n_rows):
        value = value + whole_in[k - 1]
    series_buf[...] = value

    @pl.when(at_edge)
    def _():
        whole_wait(last_in, recv_sem.at[6]).wait_recv()
        for k in range(1, n_cols):
            latest_buf[lax.rem(col + n_cols - k, n_cols)] = last_in[k - 1]
        latest = jnp.concatenate([latest_buf[d] for d in range(n_cols)], axis=1)
        high, rest = split(latest)
        middle, rest = split(rest)
        parts = jnp.concatenate([high.astype(F32), middle.astype(F32), rest, rest], axis=0)
        picked = lax.dot_general(
            parts.astype(BF16), chosen_buf[...], (((1,), (1,)), ((), ())),
            preferred_element_type=F32,
        )
        picked = picked[0:2] + picked[2:4] + picked[4:6]
        base = tall - 2 * EDGE
        part_rows = pl.ds(base, 3 * EDGE)
        at_ghost = lax.broadcasted_iota(jnp.int32, (3 * EDGE, span), 0) == 2 * EDGE
        ghosts = [
            jnp.broadcast_to(picked[k:k + 1], (3 * EDGE, span)) for k in range(2)
        ]
        wet, speed_sq = pad[4, part_rows], pad[3, part_rows]
        speed = jnp.sqrt(speed_sq)
        face_x, face_y = faces(speed, wet, 1), faces(speed, wet, 0)
        surf = jnp.where(at_ghost, ghosts[0], pad[0, part_rows])
        surf, qx, qy = step_once(
            surf, pad[1, part_rows], pad[2, part_rows], speed_sq, wet, face_x, face_y
        )
        surf = jnp.where(at_ghost, ghosts[1], surf)
        qx = jnp.where(at_ghost, 0.0, qx)
        qy = jnp.where(at_ghost, 0.0, qy)
        new = step_once(surf, qx, qy, speed_sq, wet, face_x, face_y)
        for k in range(3):
            out_buf[k, tall - EDGE:] = new[k][EDGE:2 * EDGE, :wide]

    for exists, _, copy in moves:
        @pl.when(exists)
        def _(copy=copy):
            copy.wait_send()
    for ref, sem in (
        (part.at[:, 0], send_sem.at[0]), (late_in, send_sem.at[1]), (y_in, send_sem.at[2]),
        (z_in, send_sem.at[3]), (whole_in, send_sem.at[4]),
    ):
        whole_wait(ref, sem).wait_send()
    for h in range(Z_HIGH):
        @pl.when(jnp.logical_not(at_edge & (z_high == h)))
        def _(h=h):
            whole_wait(late_out.at[h], late_send.at[h]).wait_send()

    @pl.when(at_edge)
    def _():
        whole_wait(last_in, send_sem.at[5]).wait_send()


def write_out(series, fields, series_hbm, surf_hbm, qx_hbm, qy_hbm, sems):
    copies = [pltpu.make_async_copy(series, series_hbm, sems.at[3])]
    for k, target in enumerate((surf_hbm, qx_hbm, qy_hbm)):
        copies.append(pltpu.make_async_copy(fields.at[k], target, sems.at[k]))
    for copy in copies:
        copy.start()
    for copy in copies:
        copy.wait()


def on_device(n_rows, n_cols, kernel_hat, coefficients, wave_speed_sq, wet_mask, boundary_cell, height, flux_x, flux_y):
    _, freqs, src, obs = kernel_hat.shape
    steps = coefficients.shape[0]
    tall, wide = height.shape
    points = obs // n_cols
    own_steps = steps // n_rows
    span = wide + LANE
    forward, inverse = tables(freqs * n_rows, steps, n_rows)
    dma = pltpu.SemaphoreType.DMA
    anywhere = pl.BlockSpec(memory_space=pltpu.HBM)
    in_vmem = pl.BlockSpec(memory_space=pltpu.VMEM)
    series, fields = pl.pallas_call(
        functools.partial(kernel, n_rows, n_cols),
        out_shape=(
            pltpu.VMEM((own_steps, points), F32),
            pltpu.VMEM((3, tall, wide), F32),
        ),
        in_specs=[anywhere] * 10,
        out_specs=(in_vmem,) * 2,
        scratch_shapes=[
            pltpu.VMEM((Y, 2, freqs, src, obs // Y), BF16),
            pltpu.VMEM((src, steps), F32),
            pltpu.VMEM(forward.shape[1:], F32),
            pltpu.VMEM(inverse.shape[1:], BF16),
            pltpu.VMEM((1, obs), jnp.int32),
            pltpu.VMEM((5, tall + 2 * EDGE, span), F32),
            pltpu.VMEM((tall, wide), jnp.int32),
            pltpu.VMEM((4, 5, EDGE, LANE), F32),
            pltpu.VMEM((32, tall), F32),
            pltpu.VMEM((32, tall), F32),
            pltpu.VMEM((Y, CORES, Z_HIGH, 2 * freqs, points), F32),
            pltpu.VMEM((Y, Z_HIGH, 2 * freqs, points), F32),
            pltpu.VMEM((Y - 1, Z_HIGH, 2 * freqs, points), F32),
            pltpu.VMEM((Y - 1, Z_HIGH, 2 * freqs, points), F32),
            pltpu.VMEM((Z_HIGH, 2 * freqs, points), F32),
            pltpu.VMEM((2 * freqs, points), F32),
            pltpu.VMEM((steps, points), F32),
            pltpu.VMEM((n_rows - 1, own_steps, points), F32),
            pltpu.VMEM((Y, CORES, Z_HIGH, 2, points), F32),
            pltpu.VMEM((Y * CORES - 1, Z_HIGH, 2, points), F32),
            pltpu.VMEM((Z_HIGH, 2, points), F32),
            pltpu.VMEM((X * Z_LOW * Z_HIGH - 1, 2, points), F32),
            pltpu.VMEM((2, points), F32),
            pltpu.VMEM((n_cols - 1, 2, points), F32),
            pltpu.VMEM((n_cols, 2, points), F32),
            pltpu.VMEM((3, tall + 2 * EDGE, span), F32),
            pltpu.VMEM((span, obs), BF16),
            dma((9,)),
            dma((Y, 2)),
            dma((Y,)),
            dma((8,)),
            dma((8,)),
            dma((Z_HIGH,)),
            dma((6,)),
            dma((7,)),
        ],
        compiler_params=pltpu.CompilerParams(
            collective_id=0, has_side_effects=True, vmem_limit_bytes=60 * 1024 * 1024
        ),
    )(
        kernel_hat, coefficients.T, wave_speed_sq, wet_mask, boundary_cell.reshape(1, obs),
        height, flux_x, flux_y, jnp.asarray(forward), jnp.asarray(inverse),
    )
    return pl.pallas_call(
        write_out,
        out_shape=(
            jax.ShapeDtypeStruct((own_steps, points), F32),
            jax.ShapeDtypeStruct((tall, wide), F32),
            jax.ShapeDtypeStruct((tall, wide), F32),
            jax.ShapeDtypeStruct((tall, wide), F32),
        ),
        in_specs=[in_vmem] * 2,
        out_specs=(anywhere,) * 4,
        scratch_shapes=[dma((4,))],
        compiler_params=pltpu.CompilerParams(vmem_limit_bytes=4 * 1024 * 1024),
    )(series, fields)


def solution(mesh):
    n_rows, n_cols = mesh.shape["rows"], mesh.shape["cols"]
    return jax.shard_map(
        functools.partial(on_device, n_rows, n_cols),
        mesh=mesh,
        in_specs=(
            P(None, "rows", "cols", None),
            P(None, "cols"),
            P("rows", "cols"),
            P("rows", "cols"),
            P(),
            P("rows", "cols"),
            P("rows", "cols"),
            P("rows", "cols"),
        ),
        out_specs=(P("rows", "cols"), P("rows", "cols"), P("rows", "cols"), P("rows", "cols")),
        check_vma=False,
    )
```

profile of v0, /device:TPU:103, one launch (start us, length us, event | category | flops | bytes accessed | tf_op | source)
XLA Modules:
  0.0 30.4 jit_solution(3538155455216294761)
XLA Ops:
  0.6 28.8 %shard_map.129 = (f32[8,256]{1,0:T(8,128)S(1)}, f32[3,256,256]{2,1,0:T(8,128)S(1)}) custom-call(bf16[2,16,32,4096]{3,2,1,0:T(8,128)(2,1)} %kern_hbm.1, f32[32,128]{1,0:T(8,128)} %bitcast.2, f32[256,256]{1,0:T(8,128)} %sq_hbm.1, s32[256,256]{1,0:T(8,128)} %wet_hbm.1, s32[1,4096]{1,0:T(1,128)} %bitcast.3, f32[256,256]{1,0:T(8,128)} %surf_hbm.1, ...), custom_call_target="tpu_custom_call" | custom-call | tf_op jit(solution)/shard_map/pallas_call | solution.py:475
  29.5 0.9 %shard_map.130 = (f32[8,256]{1,0:T(8,128)}, f32[256,256]{1,0:T(8,128)}, f32[256,256]{1,0:T(8,128)}, f32[256,256]{1,0:T(8,128)}) custom-call(f32[8,256]{1,0:T(8,128)S(1)} %get-tuple-element.6.series, f32[3,256,256]{2,1,0:T(8,128)S(1)} %get-tuple-element.7.fields), custom_call_target="tpu_custom_call" | custom-call | tf_op jit(solution)/shard_map/pallas_call | solution.py:527
where the time goes:
time: 30.6 us; the launch traced here: 30.4 us
  Pallas kernels  29.8 us (97%)
  between operations  0.64 us (2%)
    pallas_call x1, Pallas kernels, on_device(): pl.pallas_call(functools.partial(kernel, n_rows, n_cols), out_shape=(pltp...  28.8 us
    pallas_call x1, Pallas kernels, on_device(): pl.pallas_call(write_out, out_shape=(jax.ShapeDtypeStruct((own_steps, poi...  0.92 us

commit v1 on v0

--- a/solution.py
+++ b/solution.py
@@ -13,11 +13,17 @@
 GROUP = 8
 X, Y, Z_LOW, Z_HIGH, CORES = 4, 4, 4, 2, 2
 Y_ORDER = (2, 1, 3, 0)
-BARRIER_AFTER = 3
+BARRIER_AFTER = 2
 EDGE = 8
 LANE = 128
 F32 = jnp.float32
 BF16 = jnp.bfloat16
+
+
+def halves(table):
+    high = table.astype(np.float32).astype(jnp.bfloat16)
+    low = (table - high.astype(np.float64)).astype(np.float32).astype(jnp.bfloat16)
+    return np.concatenate([high, high, low], axis=2)
 
 
 def tables(freq_total, steps, row_devs):
@@ -29,9 +35,8 @@
     both = np.concatenate([cos, -sin], axis=2).reshape(row_devs, -1, steps)
     forward = both.astype(np.float32)
     inverse = np.swapaxes(both, 1, 2) / freq_total
-    high = inverse.astype(np.float32).astype(jnp.bfloat16)
-    low = (inverse - high.astype(np.float64)).astype(np.float32).astype(jnp.bfloat16)
-    return forward, np.concatenate([high, high, low], axis=2)
+    four = np.swapaxes(both.reshape(row_devs // X, -1, steps), 1, 2) / freq_total
+    return forward, halves(inverse[:, steps - 2 * GROUP:]), halves(four)
 
 
 def split(value):
@@ -65,12 +70,12 @@
 
 def kernel(
     n_rows, n_cols,
-    kern_hbm, coef_hbm, sq_hbm, wet_hbm, cell_hbm, surf_hbm, qx_hbm, qy_hbm, fwd_hbm, inv_hbm,
+    kern_hbm, coef_hbm, sq_hbm, wet_hbm, cell_hbm, surf_hbm, qx_hbm, qy_hbm, fwd_hbm, tail_hbm, inv_hbm,
     series_buf, out_buf,
-    kern, coef, fwd, inv, cells, pad, wet_int, corner, strip_out, strip_in,
-    part, core_in, y_out, y_in, z_out, z_in, whole_buf, whole_in,
-    late_part, late_in, late_out, edge_in, last_out, last_in, latest_buf, mid, chosen_buf,
-    local_sem, kern_sem, core_recv, halo_send, halo_recv, late_send, send_sem, recv_sem,
+    kern, coef, fwd, tail, inv, cells, pad, wet_int, corner, strip_out, strip_in,
+    part, core_in, plane_out, plane_in, spec_buf, whole_buf, whole_in,
+    late_part, late_in, late_out, edge_in, mid, chosen_buf,
+    local_sem, kern_sem, core_recv, halo_send, halo_recv, send_sem, recv_sem,
 ):
     row = lax.axis_index("rows")
     col = lax.axis_index("cols")
@@ -88,19 +93,17 @@
     has_w, has_e = col > 0, col < n_cols - 1
     at_edge = row == n_rows - 1
 
-    def column(y_at, z_high_at, core_at):
-        return (y_at * Z_HIGH + z_high_at) * CORES + core_at
-
     inputs = [
         pltpu.make_async_copy(coef_hbm, coef, local_sem.at[0]),
         pltpu.make_async_copy(fwd_hbm.at[row], fwd, local_sem.at[1]),
-        pltpu.make_async_copy(inv_hbm.at[row], inv, local_sem.at[2]),
+        pltpu.make_async_copy(tail_hbm.at[row], tail, local_sem.at[2]),
         pltpu.make_async_copy(surf_hbm, pad.at[0, :tall, :wide], local_sem.at[3]),
         pltpu.make_async_copy(qx_hbm, pad.at[1, :tall, :wide], local_sem.at[4]),
         pltpu.make_async_copy(qy_hbm, pad.at[2, :tall, :wide], local_sem.at[5]),
         pltpu.make_async_copy(sq_hbm, pad.at[3, :tall, :wide], local_sem.at[6]),
         pltpu.make_async_copy(wet_hbm, wet_int, local_sem.at[7]),
-        pltpu.make_async_copy(cell_hbm, cells, local_sem.at[8]),
+        pltpu.make_async_copy(inv_hbm.at[z_low], inv, local_sem.at[8]),
+        pltpu.make_async_copy(cell_hbm, cells, local_sem.at[9]),
     ]
     for copy in inputs[:3]:
         copy.start()
@@ -113,41 +116,52 @@
             )
             copy.start()
             chunks.append(copy)
-    for copy in inputs[3:]:
-        copy.start()
 
     diagonals = [
         (has_n & has_w, -1, -1), (has_n & has_e, -1, 1),
         (has_s & has_w, 1, -1), (has_s & has_e, 1, 1),
     ]
-    plane = [(dy, dc) for dy in range(Y) for dc in range(CORES) if dy or dc]
+    plane = [
+        (dy, dx, dc) for dy in range(Y) for dx in range(X) for dc in range(CORES) if dy or dx or dc
+    ]
+    depth = Z_LOW * Z_HIGH
+    home = x // Z_HIGH == z_high
     barrier = pltpu.get_barrier_semaphore()
 
     def greet(to):
         pl.semaphore_signal(barrier, 1, device_id=to, device_id_type=MESH)
 
-    def beside_me(dy, dc):
-        return (row, column(lax.rem(y + dy, Y), z_high, lax.rem(core + dc, CORES)))
-
-    partner_z = (row, column(y, 1 - z_high, core))
-    partner_core = (row, column(y, z_high, 1 - core))
-    for k in range(1, n_rows):
-        greet((lax.rem(row + k, n_rows), col))
-    greet(partner_z)
-    for dy, dc in plane:
-        greet(beside_me(dy, dc))
-    sides = [(has_w, 0, -1), (has_e, 0, 1)] + diagonals
+    def device(x_at, y_at, z_at, core_at):
+        return (
+            lax.rem(z_at, Z_LOW) * X + x_at,
+            (y_at * Z_HIGH + z_at // Z_LOW) * CORES + core_at,
+        )
+
+    def in_plane(dy, dx, dc):
+        return device(lax.rem(x + dx, X), lax.rem(y + dy, Y), z, lax.rem(core + dc, CORES))
+
+    partner_core = device(x, y, z, 1 - core)
+
+    @pl.when(at_edge)
+    def _():
+        for dz in range(1, depth):
+            greet(device(x, y, lax.rem(z + dz, depth), core))
+    for dz in (4, 3, 5, 2, 6, 1, 7):
+        for half in range(2):
+            greet(device(z_high * 2 + half, y, lax.rem(z + dz, depth), core))
+    for half in range(2):
+        @pl.when(x != z_high * 2 + half)
+        def _(half=half):
+            greet(device(z_high * 2 + half, y, z, core))
+    for dy, dx, dc in plane:
+        greet(in_plane(dy, dx, dc))
+    sides = [(has_n, -1, 0), (has_s, 1, 0), (has_w, 0, -1), (has_e, 0, 1)] + diagonals
     for exists, dr, dc in sides:
         @pl.when(exists)
         def _(dr=dr, dc=dc):
             greet((row + dr, col + dc))
-
-    @pl.when(at_edge)
-    def _():
-        for r in range(n_rows - 1):
-            greet((r, partner_z[1]))
-        for k in range(1, n_cols):
-            greet((row, lax.rem(col + k, n_cols)))
+    for copy in inputs[3:]:
+        copy.start()
 
     def remote(source, target, send, recv, to):
         return pltpu.make_async_remote_copy(
@@ -185,15 +199,14 @@
         remote(
             part.at[i, 1 - core], core_in.at[i], send_sem.at[0], core_recv.at[i], partner_core
         ).start()
-        for k, (dy, dc) in enumerate(plane):
+        for k, (dy, dx, dc) in enumerate(plane):
             if dy == Y_ORDER[i]:
                 remote(
-                    late_part.at[i, lax.rem(core + dc, CORES)], late_in.at[k],
-                    send_sem.at[1], recv_sem.at[1], beside_me(dy, dc),
+                    late_part.at[i, lax.rem(core + dc, CORES), lax.rem(x + dx, X)], late_in.at[k],
+                    send_sem.at[1], recv_sem.at[0], in_plane(dy, dx, dc),
                 ).start()
 
     inputs[2].wait()
-    late_rows = inv[inv.shape[0] - 2 * GROUP:]
     for i in range(Y):
         chunks[2 * i].wait()
         chunks[2 * i + 1].wait()
@@ -208,18 +221,20 @@
         total = jnp.concatenate(totals, axis=0)
         high, low = split(total)
         late = jnp.dot(
-            late_rows, jnp.concatenate([high, low.astype(BF16), high], axis=0),
+            tail[...], jnp.concatenate([high, low.astype(BF16), high], axis=0),
             preferred_element_type=F32,
         )[2 * GROUP - 2:]
         for h in range(Z_HIGH):
             for c in range(CORES):
-                at = (h * CORES + c) * points
-                part[i, c, h] = total[:, at:at + points]
-                late_part[i, c, h] = late[:, at:at + points]
+                for half in range(2):
+                    at = (h * CORES + c) * points + half * LANE
+                    part[i, c, 2 * h + half] = total[:, at:at + LANE]
+                    late_part[i, c, 2 * h + half] = late[:, at:at + LANE]
         if i == BARRIER_AFTER:
             pl.semaphore_wait(
                 barrier,
-                n_rows - 1 + 1 + len(plane) + jnp.where(at_edge, n_cols - 1, 1)
+                len(plane) + 2 * depth - home.astype(jnp.int32)
+                + jnp.where(x == X - 1, 2 - at_edge.astype(jnp.int32), 0)
                 + sum(exists.astype(jnp.int32) for exists, _, _ in sides),
             )
             for j in range(i + 1):
@@ -245,12 +260,13 @@
 
     for i in range(Y):
         whole_wait(core_in.at[i], core_recv.at[i]).wait_recv()
-        if Y_ORDER[i]:
-            y_out[i] = part[i, core] + core_in[i]
-            remote(
-                y_out.at[i], y_in.at[i], send_sem.at[2], recv_sem.at[2],
-                (row, column(lax.rem(y + Y_ORDER[i], Y), z_high, core)),
-            ).start()
+        plane_out[i] = part[i, core] + core_in[i]
+        for dx in (2, 1, 3, 0):
+            if Y_ORDER[i] or dx:
+                remote(
+                    plane_out.at[i, lax.rem(x + dx, X)], plane_in.at[(i + 1) % Y * X + dx],
+                    send_sem.at[2], recv_sem.at[1], in_plane(Y_ORDER[i], dx, 0),
+                ).start()
 
     north = (lax.rem(row + n_rows - 1, n_rows), col)
     south = (lax.rem(row + 1, n_rows), col)
@@ -282,28 +298,63 @@
         def _(copy=copy):
             copy.start()
 
-    whole_wait(late_in, recv_sem.at[1]).wait_recv()
-    late = late_part[Y - 1, core]
+    whole_wait(late_in, recv_sem.at[0]).wait_recv()
+    late = late_part[Y - 1, core, x]
     for k in range(len(plane)):
         late = late + late_in[k]
     late_out[...] = late
-    for h in range(Z_HIGH):
-        @pl.when(jnp.logical_not(at_edge & (z_high == h)))
-        def _(h=h):
-            ahead = lax.rem(h * Z_LOW + Z_LOW - 1 - z + Z_LOW * Z_HIGH, Z_LOW * Z_HIGH)
-            slot = lax.max(ahead * X + X - 1 - x - 1, 0)
+    block = ((y * Z_HIGH + x // 2) * CORES + core) * 2 + lax.rem(x, 2)
+    blocks = obs // LANE
+    for k in range(n_cols):
+        def _(k=k):
             remote(
-                late_out.at[h], edge_in.at[slot], late_send.at[h], recv_sem.at[3],
-                (n_rows - 1, column(y, h, core)),
+                late_out, edge_in.at[z * blocks + block], send_sem.at[3], recv_sem.at[2],
+                (n_rows - 1, lax.rem(col + k, n_cols)),
             ).start()
-
-    whole_wait(y_in, recv_sem.at[2]).wait_recv()
-    value = part[Y - 1, core] + core_in[Y - 1]
-    for i in range(Y - 1):
-        value = value + y_in[i]
-    z_out[...] = value
-    z_copy = remote(z_out.at[1 - z_high], z_in, send_sem.at[3], recv_sem.at[4], partner_z)
-    z_copy.start()
+        if k:
+            _()
+        else:
+            pl.when(jnp.logical_not(at_edge))(_)
+
+    @pl.when(at_edge)
+    def _():
+        edge_in[z * blocks + block] = late
+
+    others = plane_in.at[pl.ds(1, X * Y - 1)]
+    whole_wait(others, recv_sem.at[1]).wait_recv()
+    for dx in range(X):
+        value = plane_out[Y - 1, x] if dx == 0 else plane_in[dx]
+        for i in range(Y - 1):
+            value = value + plane_in[(i + 1) * X + dx]
+        spec_buf[lax.rem(x + X - dx, X)] = value
+    inputs[8].wait()
+    high, low = split(spec_buf[...].reshape(X * 2 * freqs, LANE))
+    whole = jnp.dot(
+        inv[...], jnp.concatenate([high, low.astype(BF16), high], axis=0),
+        preferred_element_type=F32,
+    )
+    whole_buf[...] = whole
+    z_base = x // 2 * Z_LOW
+    own_half = lax.rem(x, 2) * depth
+    for k in range(n_rows):
+        def _(k=k):
+            to = lax.rem(row + k, n_rows)
+            z_to = z_base + to // X
+            remote(
+                whole_buf.at[pl.ds(pl.multiple_of(to * own_steps, own_steps), own_steps)],
+                whole_in.at[own_half + lax.rem(z_to - z + depth, depth)],
+                send_sem.at[4], recv_sem.at[3], device(lax.rem(to, X), y, z_to, core),
+            ).start()
+        if k:
+            _()
+        else:
+            pl.when(jnp.logical_not(home))(_)
+
+    @pl.when(home)
+    def _():
+        whole_in[own_half] = whole_buf[
+            pl.ds(pl.multiple_of(row * own_steps, own_steps), own_steps)
+        ]
 
     for i, (_, arrives, copy) in enumerate(moves):
         @pl.when(arrives)
@@ -356,54 +407,38 @@
 
     first_step()
 
-    whole_wait(z_in, recv_sem.at[4]).wait_recv()
-    high, low = split(z_out[z_high] + z_in[...])
-    whole = jnp.dot(
-        inv[...], jnp.concatenate([high, low.astype(BF16), high], axis=0),
-        preferred_element_type=F32,
-    )
-    whole_buf[...] = whole
-    for k in range(1, n_rows):
-        to = lax.rem(row + k, n_rows)
-        remote(
-            whole_buf.at[pl.ds(pl.multiple_of(to * own_steps, own_steps), own_steps)],
-            whole_in.at[k - 1], send_sem.at[4], recv_sem.at[5], (to, col),
-        ).start()
-
-    inputs[8].wait()
+    inputs[9].wait()
     span = wide + LANE
 
     @pl.when(at_edge)
     def _():
-        whole_wait(edge_in, recv_sem.at[3]).wait_recv()
-        value = late_out[z_high]
-        for k in range(Z_LOW * Z_HIGH * X - 1):
-            value = value + edge_in[k]
-        last_out[...] = value
-        latest_buf[col] = value
-        for k in range(1, n_cols):
-            remote(
-                last_out, last_in.at[k - 1], send_sem.at[5], recv_sem.at[6],
-                (row, lax.rem(col + k, n_cols)),
-            ).start()
         place = lax.broadcasted_iota(jnp.int32, (span, obs), 0)
         place = jnp.where(place >= wide + LANE // 2, place - span, place) + col * wide
         chosen_buf[...] = jnp.where(place == cells[...], 1.0, 0.0).astype(BF16)
 
     second_step()
 
-    whole_wait(whole_in, recv_sem.at[5]).wait_recv()
-    value = whole_buf[pl.ds(pl.multiple_of(row * own_steps, own_steps), own_steps)]
-    for k in range(1, n_rows):
-        value = value + whole_in[k - 1]
-    series_buf[...] = value
+    @pl.when(home)
+    def _():
+        whole_wait(whole_in.at[pl.ds(0, 2 * depth - 1)], recv_sem.at[3]).wait_recv()
+
+    @pl.when(jnp.logical_not(home))
+    def _():
+        whole_wait(whole_in, recv_sem.at[3]).wait_recv()
+
+    for half in range(2):
+        value = whole_in[half * depth]
+        for k in range(1, depth):
+            value = value + whole_in[half * depth + k]
+        series_buf[:, half * LANE:(half + 1) * LANE] = value
 
     @pl.when(at_edge)
     def _():
-        whole_wait(last_in, recv_sem.at[6]).wait_recv()
-        for k in range(1, n_cols):
-            latest_buf[lax.rem(col + n_cols - k, n_cols)] = last_in[k - 1]
-        latest = jnp.concatenate([latest_buf[d] for d in range(n_cols)], axis=1)
+        whole_wait(edge_in.at[pl.ds(0, depth * blocks - 1)], recv_sem.at[2]).wait_recv()
+        total = edge_in[pl.ds(0, blocks)]
+        for k in range(1, depth):
+            total = total + edge_in[pl.ds(k * blocks, blocks)]
+        latest = jnp.concatenate([total[b] for b in range(blocks)], axis=1)
         high, rest = split(latest)
         middle, rest = split(rest)
         parts = jnp.concatenate([high.astype(F32), middle.astype(F32), rest, rest], axis=0)
@@ -437,18 +472,26 @@
         def _(copy=copy):
             copy.wait_send()
     for ref, sem in (
-        (part.at[:, 0], send_sem.at[0]), (late_in, send_sem.at[1]), (y_in, send_sem.at[2]),
-        (z_in, send_sem.at[3]), (whole_in, send_sem.at[4]),
+        (core_in, send_sem.at[0]), (late_in, send_sem.at[1]),
+        (others, send_sem.at[2]),
     ):
         whole_wait(ref, sem).wait_send()
-    for h in range(Z_HIGH):
-        @pl.when(jnp.logical_not(at_edge & (z_high == h)))
-        def _(h=h):
-            whole_wait(late_out.at[h], late_send.at[h]).wait_send()
 
     @pl.when(at_edge)
     def _():
-        whole_wait(last_in, send_sem.at[5]).wait_send()
+        whole_wait(edge_in.at[pl.ds(0, n_cols - 1)], send_sem.at[3]).wait_send()
+
+    @pl.when(jnp.logical_not(at_edge))
+    def _():
+        whole_wait(edge_in.at[pl.ds(0, n_cols)], send_sem.at[3]).wait_send()
+
+    @pl.when(home)
+    def _():
+        whole_wait(whole_in.at[pl.ds(0, 2 * depth - 1)], send_sem.at[4]).wait_send()
+
+    @pl.when(jnp.logical_not(home))
+    def _():
+        whole_wait(whole_in, send_sem.at[4]).wait_send()
 
 
 def write_out(series, fields, series_hbm, surf_hbm, qx_hbm, qy_hbm, sems):
@@ -468,7 +511,7 @@
     points = obs // n_cols
     own_steps = steps // n_rows
     span = wide + LANE
-    forward, inverse = tables(freqs * n_rows, steps, n_rows)
+    forward, tail, inverse = tables(freqs * n_rows, steps, n_rows)
     dma = pltpu.SemaphoreType.DMA
     anywhere = pl.BlockSpec(memory_space=pltpu.HBM)
     in_vmem = pl.BlockSpec(memory_space=pltpu.VMEM)
@@ -478,12 +521,13 @@
             pltpu.VMEM((own_steps, points), F32),
             pltpu.VMEM((3, tall, wide), F32),
         ),
-        in_specs=[anywhere] * 10,
+        in_specs=[anywhere] * 11,
         out_specs=(in_vmem,) * 2,
         scratch_shapes=[
             pltpu.VMEM((Y, 2, freqs, src, obs // Y), BF16),
             pltpu.VMEM((src, steps), F32),
             pltpu.VMEM(forward.shape[1:], F32),
+            pltpu.VMEM(tail.shape[1:], BF16),
             pltpu.VMEM(inverse.shape[1:], BF16),
             pltpu.VMEM((1, obs), jnp.int32),
             pltpu.VMEM((5, tall + 2 * EDGE, span), F32),
@@ -491,38 +535,34 @@
             pltpu.VMEM((4, 5, EDGE, LANE), F32),
             pltpu.VMEM((32, tall), F32),
             pltpu.VMEM((32, tall), F32),
-            pltpu.VMEM((Y, CORES, Z_HIGH, 2 * freqs, points), F32),
-            pltpu.VMEM((Y, Z_HIGH, 2 * freqs, points), F32),
-            pltpu.VMEM((Y - 1, Z_HIGH, 2 * freqs, points), F32),
-            pltpu.VMEM((Y - 1, Z_HIGH, 2 * freqs, points), F32),
-            pltpu.VMEM((Z_HIGH, 2 * freqs, points), F32),
-            pltpu.VMEM((2 * freqs, points), F32),
-            pltpu.VMEM((steps, points), F32),
-            pltpu.VMEM((n_rows - 1, own_steps, points), F32),
-            pltpu.VMEM((Y, CORES, Z_HIGH, 2, points), F32),
-            pltpu.VMEM((Y * CORES - 1, Z_HIGH, 2, points), F32),
-            pltpu.VMEM((Z_HIGH, 2, points), F32),
-            pltpu.VMEM((X * Z_LOW * Z_HIGH - 1, 2, points), F32),
-            pltpu.VMEM((2, points), F32),
-            pltpu.VMEM((n_cols - 1, 2, points), F32),
-            pltpu.VMEM((n_cols, 2, points), F32),
+            pltpu.VMEM((Y, CORES, X, 2 * freqs, LANE), F32),
+            pltpu.VMEM((Y, X, 2 * freqs, LANE), F32),
+            pltpu.VMEM((Y, X, 2 * freqs, LANE), F32),
+            pltpu.VMEM((Y * X, 2 * freqs, LANE), F32),
+            pltpu.VMEM((X, 2 * freqs, LANE), F32),
+            pltpu.VMEM((steps, LANE), F32),
+            pltpu.VMEM((2 * Z_LOW * Z_HIGH, own_steps, LANE), F32),
+            pltpu.VMEM((Y, CORES, X, 2, LANE), F32),
+            pltpu.VMEM((Y * X * CORES - 1, 2, LANE), F32),
+            pltpu.VMEM((2, LANE), F32),
+            pltpu.VMEM((Z_LOW * Z_HIGH * (obs // LANE), 2, LANE), F32),
             pltpu.VMEM((3, tall + 2 * EDGE, span), F32),
             pltpu.VMEM((span, obs), BF16),
-            dma((9,)),
+            dma((10,)),
             dma((Y, 2)),
             dma((Y,)),
             dma((8,)),
             dma((8,)),
-            dma((Z_HIGH,)),
-            dma((6,)),
-            dma((7,)),
+            dma((5,)),
+            dma((4,)),
         ],
         compiler_params=pltpu.CompilerParams(
             collective_id=0, has_side_effects=True, vmem_limit_bytes=60 * 1024 * 1024
         ),
     )(
         kernel_hat, coefficients.T, wave_speed_sq, wet_mask, boundary_cell.reshape(1, obs),
-        height, flux_x, flux_y, jnp.asarray(forward), jnp.asarray(inverse),
+        height, flux_x, flux_y, jnp.asarray(forward), jnp.asarray(tail),
+        jnp.asarray(inverse),
     )
     return pl.pallas_call(
         write_out,

time: 30.6 us -> 27.2 us (0.89)
  the two profiles are of different devices: /device:TPU:103 before, /device:TPU:6 now
where the time goes in v1:
time: 27.2 us; the launch traced here: 27.1 us
  Pallas kernels  26.5 us (97%)
  between operations  0.64 us (2%)
    pallas_call x1, Pallas kernels, on_device(): pl.pallas_call(functools.partial(kernel, n_rows, n_cols), out_shape=(pltp...  25.6 us
    pallas_call x1, Pallas kernels, on_device(): pl.pallas_call(write_out, out_shape=(jax.ShapeDtypeStruct((own_steps, poi...  0.92 us

profile of v1, /device:TPU:6, one launch (start us, length us, event | category | flops | bytes accessed | tf_op | source)
XLA Modules:
  0.0 27.1 jit_solution(8572031091756022359)
XLA Ops:
  0.6 25.6 %shard_map.138 = (f32[8,256]{1,0:T(8,128)S(1)}, f32[3,256,256]{2,1,0:T(8,128)S(1)}) custom-call(bf16[2,16,32,4096]{3,2,1,0:T(8,128)(2,1)} %kern_hbm.1, f32[32,128]{1,0:T(8,128)} %bitcast.2, f32[256,256]{1,0:T(8,128)} %sq_hbm.1, s32[256,256]{1,0:T(8,128)} %wet_hbm.1, s32[1,4096]{1,0:T(1,128)} %bitcast.3, f32[256,256]{1,0:T(8,128)} %surf_hbm.1, ...), custom_call_target="tpu_custom_call" | custom-call | tf_op jit(solution)/shard_map/pallas_call | solution.py:518
  26.2 0.9 %shard_map.139 = (f32[8,256]{1,0:T(8,128)}, f32[256,256]{1,0:T(8,128)}, f32[256,256]{1,0:T(8,128)}, f32[256,256]{1,0:T(8,128)}) custom-call(f32[8,256]{1,0:T(8,128)S(1)} %get-tuple-element.6.series, f32[3,256,256]{2,1,0:T(8,128)S(1)} %get-tuple-element.7.fields), custom_call_target="tpu_custom_call" | custom-call | tf_op jit(solution)/shard_map/pallas_call | solution.py:567

commit v2 on v1

--- a/solution.py
+++ b/solution.py
@@ -11,9 +11,10 @@
 
 MESH = pl.DeviceIdType.MESH
 GROUP = 8
+REACH = 2
 X, Y, Z_LOW, Z_HIGH, CORES = 4, 4, 4, 2, 2
 Y_ORDER = (2, 1, 3, 0)
-BARRIER_AFTER = 2
+BARRIER_AFTER = 1
 EDGE = 8
 LANE = 128
 F32 = jnp.float32
@@ -36,7 +37,9 @@
     forward = both.astype(np.float32)
     inverse = np.swapaxes(both, 1, 2) / freq_total
     four = np.swapaxes(both.reshape(row_devs // X, -1, steps), 1, 2) / freq_total
-    return forward, halves(inverse[:, steps - 2 * GROUP:]), halves(four)
+    late = halves(inverse[:, steps - 2 * GROUP:]).astype(np.float32)
+    late = np.pad(late, ((0, 0), (0, 0), (0, steps - late.shape[2])))
+    return np.concatenate([forward, late], axis=1), halves(four)
 
 
 def split(value):
@@ -44,38 +47,43 @@
     return high, value - high.astype(F32)
 
 
-def faces(speed, wet, dim):
-    ahead = speed.shape[dim] - 1
-    opened = wet * pltpu.roll(wet, ahead, dim)
-    return 0.5 * opened, opened * (0.25 * (speed + pltpu.roll(speed, ahead, dim)))
-
-
-def step_once(surf, qx, qy, speed_sq, wet, face_x, face_y):
+def faces(speed_sq, wet):
+    speed = 0.0625 * jnp.sqrt(speed_sq)
+    found = []
+    for dim in (1, 0):
+        ahead = wet.shape[dim] - 1
+        opened = wet * pltpu.roll(wet, ahead, dim)
+        found += [0.125 * opened, opened * (speed + pltpu.roll(speed, ahead, dim))]
+    return found
+
+
+def step_once(surf, qx, qy, speed_sq, wet, face):
     energy = speed_sq * surf
     change = []
-    for dim, along, across, (half, damp) in ((1, qx, qy, face_x), (0, qy, qx, face_y)):
+    for dim, along, across, half, damp in ((1, qx, qy, *face[:2]), (0, qy, qx, *face[2:])):
         ahead = surf.shape[dim] - 1
         later = lambda v: pltpu.roll(v, ahead, dim)
-        mass = half * (along + later(along)) - damp * (later(surf) - surf)
-        momentum = half * (energy + later(energy)) - damp * (later(along) - along)
-        shear = -damp * (later(across) - across)
+        along_later = later(along)
+        mass = half * (along + along_later) + damp * (surf - later(surf))
+        momentum = half * (energy + later(energy)) + damp * (along - along_later)
+        shear = damp * (across - later(across))
         change.append([f - pltpu.roll(f, 1, dim) for f in (mass, momentum, shear)])
     (mass_x, mom_x, shear_x), (mass_y, mom_y, shear_y) = change
     return (
-        wet * (surf - 0.25 * (mass_x + mass_y)),
-        wet * (qx - 0.25 * (mom_x + shear_y)),
-        wet * (qy - 0.25 * (shear_x + mom_y)),
+        wet * (surf - (mass_x + mass_y)),
+        wet * (qx - (mom_x + shear_y)),
+        wet * (qy - (shear_x + mom_y)),
     )
 
 
 def kernel(
     n_rows, n_cols,
-    kern_hbm, coef_hbm, sq_hbm, wet_hbm, cell_hbm, surf_hbm, qx_hbm, qy_hbm, fwd_hbm, tail_hbm, inv_hbm,
+    kern_hbm, coef_hbm, sq_hbm, wet_hbm, cell_hbm, surf_hbm, qx_hbm, qy_hbm, fwd_hbm, inv_hbm,
     series_buf, out_buf,
-    kern, coef, fwd, tail, inv, cells, pad, wet_int, corner, strip_out, strip_in,
+    kern, coef, fwd, inv, cells, pad, wet_int, corner, rows_out, rows_in, strip_out, strip_in,
     part, core_in, plane_out, plane_in, spec_buf, whole_buf, whole_in,
-    late_part, late_in, late_out, edge_in, mid, chosen_buf,
-    local_sem, kern_sem, core_recv, halo_send, halo_recv, send_sem, recv_sem,
+    late_part, late_in, late_out, edge_in, face_buf, mid, chosen_buf,
+    local_sem, kern_sem, core_recv, halo_send, halo_recv, send_sem, recv_sem, near_sem, far_sem,
 ):
     row = lax.axis_index("rows")
     col = lax.axis_index("cols")
@@ -96,16 +104,15 @@
     inputs = [
         pltpu.make_async_copy(coef_hbm, coef, local_sem.at[0]),
         pltpu.make_async_copy(fwd_hbm.at[row], fwd, local_sem.at[1]),
-        pltpu.make_async_copy(tail_hbm.at[row], tail, local_sem.at[2]),
         pltpu.make_async_copy(surf_hbm, pad.at[0, :tall, :wide], local_sem.at[3]),
         pltpu.make_async_copy(qx_hbm, pad.at[1, :tall, :wide], local_sem.at[4]),
         pltpu.make_async_copy(qy_hbm, pad.at[2, :tall, :wide], local_sem.at[5]),
         pltpu.make_async_copy(sq_hbm, pad.at[3, :tall, :wide], local_sem.at[6]),
         pltpu.make_async_copy(wet_hbm, wet_int, local_sem.at[7]),
-        pltpu.make_async_copy(inv_hbm.at[z_low], inv, local_sem.at[8]),
-        pltpu.make_async_copy(cell_hbm, cells, local_sem.at[9]),
+        pltpu.make_async_copy(inv_hbm.at[z_low], inv, local_sem.at[2]),
+        pltpu.make_async_copy(cell_hbm, cells, local_sem.at[8]),
     ]
-    for copy in inputs[:3]:
+    for copy in inputs[:2]:
         copy.start()
     chunks = []
     for i, dy in enumerate(Y_ORDER):
@@ -114,8 +121,13 @@
             copy = pltpu.make_async_copy(
                 kern_hbm.at[p, :, :, pl.ds(at, per_y)], kern.at[i, p], kern_sem.at[i, p]
             )
-            copy.start()
             chunks.append(copy)
+    for copy in chunks[:2]:
+        copy.start()
+    pad[:, tall:] = jnp.zeros((5, 2 * EDGE, wide + LANE), F32)
+    rows_in[...] = jnp.zeros(rows_in.shape, F32)
+    strip_in[...] = jnp.zeros(strip_in.shape, F32)
+    corner[...] = jnp.zeros(corner.shape, F32)
 
     diagonals = [
         (has_n & has_w, -1, -1), (has_n & has_e, -1, 1),
@@ -142,25 +154,18 @@
 
     partner_core = device(x, y, z, 1 - core)
 
-    @pl.when(at_edge)
-    def _():
-        for dz in range(1, depth):
-            greet(device(x, y, lax.rem(z + dz, depth), core))
-    for dz in (4, 3, 5, 2, 6, 1, 7):
-        for half in range(2):
-            greet(device(z_high * 2 + half, y, lax.rem(z + dz, depth), core))
-    for half in range(2):
-        @pl.when(x != z_high * 2 + half)
-        def _(half=half):
-            greet(device(z_high * 2 + half, y, z, core))
+    def in_line(dz):
+        return device(x, y, lax.rem(z + dz + depth, depth), core)
+
+    for dz in (2, -2, 1, -1):
+        greet(in_line(dz))
+    for copy in chunks[2:4]:
+        copy.start()
     for dy, dx, dc in plane:
         greet(in_plane(dy, dx, dc))
-    sides = [(has_n, -1, 0), (has_s, 1, 0), (has_w, 0, -1), (has_e, 0, 1)] + diagonals
-    for exists, dr, dc in sides:
-        @pl.when(exists)
-        def _(dr=dr, dc=dc):
-            greet((row + dr, col + dc))
-    for copy in inputs[3:]:
+    for copy in chunks[4:]:
+        copy.start()
+    for copy in inputs[2:]:
         copy.start()
 
     def remote(source, target, send, recv, to):
@@ -175,7 +180,7 @@
     inputs[0].wait()
     inputs[1].wait()
     spectrum = lax.dot_general(
-        fwd[...], coef[...], (((1,), (1,)), ((), ())),
+        fwd[:2 * freqs], coef[...], (((1,), (1,)), ((), ())),
         precision=lax.Precision.HIGHEST, preferred_element_type=F32,
     )
     spread = jnp.where(
@@ -206,7 +211,7 @@
                     send_sem.at[1], recv_sem.at[0], in_plane(dy, dx, dc),
                 ).start()
 
-    inputs[2].wait()
+    tail = fwd[2 * freqs:].astype(BF16)[:, :6 * freqs]
     for i in range(Y):
         chunks[2 * i].wait()
         chunks[2 * i + 1].wait()
@@ -221,7 +226,7 @@
         total = jnp.concatenate(totals, axis=0)
         high, low = split(total)
         late = jnp.dot(
-            tail[...], jnp.concatenate([high, low.astype(BF16), high], axis=0),
+            tail, jnp.concatenate([high, low.astype(BF16), high], axis=0),
             preferred_element_type=F32,
         )[2 * GROUP - 2:]
         for h in range(Z_HIGH):
@@ -231,18 +236,34 @@
                     part[i, c, 2 * h + half] = total[:, at:at + LANE]
                     late_part[i, c, 2 * h + half] = late[:, at:at + LANE]
         if i == BARRIER_AFTER:
-            pl.semaphore_wait(
-                barrier,
-                len(plane) + 2 * depth - home.astype(jnp.int32)
-                + jnp.where(x == X - 1, 2 - at_edge.astype(jnp.int32), 0)
-                + sum(exists.astype(jnp.int32) for exists, _, _ in sides),
-            )
+            pl.semaphore_wait(barrier, len(plane) + 4)
+            for dz in (2, -2, 1, -1):
+                pl.semaphore_signal(
+                    near_sem, 1, device_id=in_line(dz), device_id_type=MESH
+                )
             for j in range(i + 1):
                 send_chunk(j)
         elif i > BARRIER_AFTER:
             send_chunk(i)
 
-    for copy in inputs[3:8]:
+    def gather(i):
+        whole_wait(core_in.at[i], core_recv.at[i]).wait_recv()
+        plane_out[i] = part[i, core] + core_in[i]
+        for dx in (2, 1, 3, 0):
+            if Y_ORDER[i] or dx:
+                remote(
+                    plane_out.at[i, lax.rem(x + dx, X)], plane_in.at[(i + 1) % Y * X + dx],
+                    send_sem.at[2], recv_sem.at[1], in_plane(Y_ORDER[i], dx, 0),
+                ).start()
+
+    gather(0)
+    gather(1)
+    pl.semaphore_wait(near_sem, 4)
+    for dz in (2, -2):
+        pl.semaphore_signal(far_sem, 1, device_id=in_line(dz), device_id_type=MESH)
+    gather(2)
+
+    for copy in inputs[2:7]:
         copy.wait()
     pad[4, :tall, :wide] = wet_int[...].astype(F32)
     lane = lax.broadcasted_iota(jnp.int32, (tall, LANE), 1)
@@ -257,41 +278,32 @@
             (lane >= at) & (lane < at + 2), pltpu.roll(last, at + 2, 1), packed
         )
     strip_out[...] = packed.T[:32]
-
-    for i in range(Y):
-        whole_wait(core_in.at[i], core_recv.at[i]).wait_recv()
-        plane_out[i] = part[i, core] + core_in[i]
-        for dx in (2, 1, 3, 0):
-            if Y_ORDER[i] or dx:
-                remote(
-                    plane_out.at[i, lax.rem(x + dx, X)], plane_in.at[(i + 1) % Y * X + dx],
-                    send_sem.at[2], recv_sem.at[1], in_plane(Y_ORDER[i], dx, 0),
-                ).start()
+    rows_out[0] = pad[:, :REACH, :wide]
+    rows_out[1] = pad[:, tall - REACH:tall, :wide]
+
+    gather(Y - 1)
+    pl.semaphore_wait(far_sem, 2)
 
     north = (lax.rem(row + n_rows - 1, n_rows), col)
     south = (lax.rem(row + 1, n_rows), col)
     west = (row, lax.rem(col + n_cols - 1, n_cols))
     east = (row, lax.rem(col + 1, n_cols))
-    top, bottom = pl.ds(0, EDGE), pl.ds(tall - EDGE, EDGE)
-    south_halo, north_halo = pl.ds(tall, EDGE), pl.ds(tall + EDGE, EDGE)
-    body = pl.ds(0, wide)
-
     def halo(source, target, i, to):
         return remote(source, target, halo_send.at[i], halo_recv.at[i], to)
 
     moves = [
-        (has_n, has_s, halo(pad.at[:, top, body], pad.at[:, south_halo, body], 0, north)),
-        (has_s, has_n, halo(pad.at[:, bottom, body], pad.at[:, north_halo, body], 1, south)),
+        (has_n, has_s, halo(rows_out.at[0], rows_in.at[0], 0, north)),
+        (has_s, has_n, halo(rows_out.at[1], rows_in.at[1], 1, south)),
         (has_w, has_e, halo(strip_out.at[pl.ds(0, 16)], strip_in.at[pl.ds(16, 16)], 2, west)),
         (has_e, has_w, halo(strip_out.at[pl.ds(16, 16)], strip_in.at[pl.ds(0, 16)], 3, east)),
     ]
     for i, (exists, dr, dc) in enumerate(diagonals):
-        rows_at = top if dr < 0 else bottom
+        side = 0 if dr < 0 else 1
         cols_at = pl.ds(0, LANE) if dc < 0 else pl.ds(wide - LANE, LANE)
         to = (lax.rem(row + dr + n_rows, n_rows), lax.rem(col + dc + n_cols, n_cols))
         moves.append((
             exists, diagonals[3 - i][0],
-            halo(pad.at[:, rows_at, cols_at], corner.at[i], 4 + i, to),
+            halo(rows_out.at[side, :, :, cols_at], corner.at[i], 4 + i, to),
         ))
     for exists, _, copy in moves:
         @pl.when(exists)
@@ -327,7 +339,7 @@
         for i in range(Y - 1):
             value = value + plane_in[(i + 1) * X + dx]
         spec_buf[lax.rem(x + X - dx, X)] = value
-    inputs[8].wait()
+    inputs[7].wait()
     high, low = split(spec_buf[...].reshape(X * 2 * freqs, LANE))
     whole = jnp.dot(
         inv[...], jnp.concatenate([high, low.astype(BF16), high], axis=0),
@@ -356,58 +368,46 @@
             pl.ds(pl.multiple_of(row * own_steps, own_steps), own_steps)
         ]
 
-    for i, (_, arrives, copy) in enumerate(moves):
+    for _, arrives, copy in moves:
         @pl.when(arrives)
         def _(copy=copy):
             copy.wait_recv()
 
-        @pl.when(jnp.logical_not(arrives))
-        def _(i=i):
-            if i == 0:
-                pad[:, south_halo, body] = jnp.zeros((5, EDGE, wide), F32)
-            elif i == 1:
-                pad[:, north_halo, body] = jnp.zeros((5, EDGE, wide), F32)
-            elif i == 2:
-                strip_in[pl.ds(16, 16)] = jnp.zeros((16, tall), F32)
-            elif i == 3:
-                strip_in[pl.ds(0, 16)] = jnp.zeros((16, tall), F32)
-            else:
-                corner[i - 4] = jnp.zeros((5, EDGE, LANE), F32)
-
     beside = jnp.concatenate([strip_in[...], jnp.zeros((LANE - 32, tall), F32)], axis=0).T
-    near = lax.broadcasted_iota(jnp.int32, (EDGE, LANE), 1) < LANE // 2
+    near = lax.broadcasted_iota(jnp.int32, (REACH, LANE), 1) < LANE // 2
+    below, above = pl.ds(tall, REACH), pl.ds(tall + 2 * EDGE - REACH, REACH)
+    pad[:, below, :wide] = rows_in[0]
+    pad[:, above, :wide] = rows_in[1]
     for k in range(5):
         pad[k, :tall, wide:] = jnp.where(
             lane < LANE // 2,
             pltpu.roll(beside, LANE - 16 - 2 * k, 1),
             pltpu.roll(beside, LANE - 2 - 2 * k, 1),
         )
-        pad[k, tall:tall + EDGE, wide:] = jnp.where(near, corner[0, k], corner[1, k])
-        pad[k, tall + EDGE:, wide:] = jnp.where(near, corner[2, k], corner[3, k])
+        pad[k, below, wide:] = jnp.where(near, corner[0, k], corner[1, k])
+        pad[k, above, wide:] = jnp.where(near, corner[2, k], corner[3, k])
 
     @pl.when(at_edge)
     def _():
         pad[3:5, tall:tall + 1, :] = jnp.ones((2, 1, wide + LANE), F32)
 
     def first_step():
-        wet, speed_sq = pad[4], pad[3]
-        speed = jnp.sqrt(speed_sq)
-        face_x, face_y = faces(speed, wet, 1), faces(speed, wet, 0)
-        new = step_once(pad[0], pad[1], pad[2], speed_sq, wet, face_x, face_y)
+        face = faces(pad[3], pad[4])
+        for k in range(4):
+            face_buf[k] = face[k]
+        new = step_once(pad[0], pad[1], pad[2], pad[3], pad[4], face)
         for k in range(3):
             mid[k] = new[k]
 
     def second_step():
-        wet, speed_sq = pad[4], pad[3]
-        speed = jnp.sqrt(speed_sq)
-        face_x, face_y = faces(speed, wet, 1), faces(speed, wet, 0)
-        new = step_once(mid[0], mid[1], mid[2], speed_sq, wet, face_x, face_y)
+        face = [face_buf[k] for k in range(4)]
+        new = step_once(mid[0], mid[1], mid[2], pad[3], pad[4], face)
         for k in range(3):
             out_buf[k] = new[k][:tall, :wide]
 
     first_step()
 
-    inputs[9].wait()
+    inputs[8].wait()
     span = wide + LANE
 
     @pl.when(at_edge)
@@ -454,16 +454,15 @@
             jnp.broadcast_to(picked[k:k + 1], (3 * EDGE, span)) for k in range(2)
         ]
         wet, speed_sq = pad[4, part_rows], pad[3, part_rows]
-        speed = jnp.sqrt(speed_sq)
-        face_x, face_y = faces(speed, wet, 1), faces(speed, wet, 0)
+        face = [face_buf[k, part_rows] for k in range(4)]
         surf = jnp.where(at_ghost, ghosts[0], pad[0, part_rows])
         surf, qx, qy = step_once(
-            surf, pad[1, part_rows], pad[2, part_rows], speed_sq, wet, face_x, face_y
+            surf, pad[1, part_rows], pad[2, part_rows], speed_sq, wet, face
         )
         surf = jnp.where(at_ghost, ghosts[1], surf)
         qx = jnp.where(at_ghost, 0.0, qx)
         qy = jnp.where(at_ghost, 0.0, qy)
-        new = step_once(surf, qx, qy, speed_sq, wet, face_x, face_y)
+        new = step_once(surf, qx, qy, speed_sq, wet, face)
         for k in range(3):
             out_buf[k, tall - EDGE:] = new[k][EDGE:2 * EDGE, :wide]
 
@@ -511,7 +510,7 @@
     points = obs // n_cols
     own_steps = steps // n_rows
     span = wide + LANE
-    forward, tail, inverse = tables(freqs * n_rows, steps, n_rows)
+    forward, inverse = tables(freqs * n_rows, steps, n_rows)
     dma = pltpu.SemaphoreType.DMA
     anywhere = pl.BlockSpec(memory_space=pltpu.HBM)
     in_vmem = pl.BlockSpec(memory_space=pltpu.VMEM)
@@ -521,18 +520,19 @@
             pltpu.VMEM((own_steps, points), F32),
             pltpu.VMEM((3, tall, wide), F32),
         ),
-        in_specs=[anywhere] * 11,
+        in_specs=[anywhere] * 10,
         out_specs=(in_vmem,) * 2,
         scratch_shapes=[
             pltpu.VMEM((Y, 2, freqs, src, obs // Y), BF16),
             pltpu.VMEM((src, steps), F32),
             pltpu.VMEM(forward.shape[1:], F32),
-            pltpu.VMEM(tail.shape[1:], BF16),
             pltpu.VMEM(inverse.shape[1:], BF16),
             pltpu.VMEM((1, obs), jnp.int32),
             pltpu.VMEM((5, tall + 2 * EDGE, span), F32),
             pltpu.VMEM((tall, wide), jnp.int32),
-            pltpu.VMEM((4, 5, EDGE, LANE), F32),
+            pltpu.VMEM((4, 5, REACH, LANE), F32),
+            pltpu.VMEM((2, 5, REACH, wide), F32),
+            pltpu.VMEM((2, 5, REACH, wide), F32),
             pltpu.VMEM((32, tall), F32),
             pltpu.VMEM((32, tall), F32),
             pltpu.VMEM((Y, CORES, X, 2 * freqs, LANE), F32),
@@ -546,23 +546,25 @@
             pltpu.VMEM((Y * X * CORES - 1, 2, LANE), F32),
             pltpu.VMEM((2, LANE), F32),
             pltpu.VMEM((Z_LOW * Z_HIGH * (obs // LANE), 2, LANE), F32),
+            pltpu.VMEM((4, tall + 2 * EDGE, span), F32),
             pltpu.VMEM((3, tall + 2 * EDGE, span), F32),
             pltpu.VMEM((span, obs), BF16),
-            dma((10,)),
+            dma((9,)),
             dma((Y, 2)),
             dma((Y,)),
             dma((8,)),
             dma((8,)),
             dma((5,)),
             dma((4,)),
+            pltpu.SemaphoreType.REGULAR,
+            pltpu.SemaphoreType.REGULAR,
         ],
         compiler_params=pltpu.CompilerParams(
             collective_id=0, has_side_effects=True, vmem_limit_bytes=60 * 1024 * 1024
         ),
     )(
         kernel_hat, coefficients.T, wave_speed_sq, wet_mask, boundary_cell.reshape(1, obs),
-        height, flux_x, flux_y, jnp.asarray(forward), jnp.asarray(tail),
-        jnp.asarray(inverse),
+        height, flux_x, flux_y, jnp.asarray(forward), jnp.asarray(inverse),
     )
     return pl.pallas_call(
         write_out,

time: 27.2 us -> 25.5 us (0.938)
  the two profiles are of different devices: /device:TPU:6 before, /device:TPU:1 now
where the time goes in v2:
time: 25.5 us; the launch traced here: 25.4 us
  Pallas kernels  24.7 us (97%)
  between operations  0.64 us (3%)
    pallas_call x1, Pallas kernels, on_device(): pl.pallas_call(functools.partial(kernel, n_rows, n_cols), out_shape=(pltp...  23.8 us
    pallas_call x1, Pallas kernels, on_device(): pl.pallas_call(write_out, out_shape=(jax.ShapeDtypeStruct((own_steps, poi...  0.92 us

profile of v2, /device:TPU:1, one launch (start us, length us, event | category | flops | bytes accessed | tf_op | source)
XLA Modules:
  0.0 25.4 jit_solution(15237142055191661027)
XLA Ops:
  0.6 23.8 %shard_map.129 = (f32[8,256]{1,0:T(8,128)S(1)}, f32[3,256,256]{2,1,0:T(8,128)S(1)}) custom-call(bf16[2,16,32,4096]{3,2,1,0:T(8,128)(2,1)} %kern_hbm.1, f32[32,128]{1,0:T(8,128)} %bitcast.2, f32[256,256]{1,0:T(8,128)} %sq_hbm.1, s32[256,256]{1,0:T(8,128)} %wet_hbm.1, s32[1,4096]{1,0:T(1,128)} %bitcast.3, f32[256,256]{1,0:T(8,128)} %surf_hbm.1, ...), custom_call_target="tpu_custom_call" | custom-call | tf_op jit(solution)/shard_map/pallas_call | solution.py:517
  24.4 0.9 %shard_map.130 = (f32[8,256]{1,0:T(8,128)}, f32[256,256]{1,0:T(8,128)}, f32[256,256]{1,0:T(8,128)}, f32[256,256]{1,0:T(8,128)}) custom-call(f32[8,256]{1,0:T(8,128)S(1)} %get-tuple-element.6.series, f32[3,256,256]{2,1,0:T(8,128)S(1)} %get-tuple-element.7.fields), custom_call_target="tpu_custom_call" | custom-call | tf_op jit(solution)/shard_map/pallas_call | solution.py:569

commit v3 on v2

--- a/solution.py
+++ b/solution.py
@@ -11,12 +11,13 @@
 
 MESH = pl.DeviceIdType.MESH
 GROUP = 8
+LANE = 128
 REACH = 2
+SHIFT = LANE // 2 + REACH
 X, Y, Z_LOW, Z_HIGH, CORES = 4, 4, 4, 2, 2
 Y_ORDER = (2, 1, 3, 0)
 BARRIER_AFTER = 1
 EDGE = 8
-LANE = 128
 F32 = jnp.float32
 BF16 = jnp.bfloat16
 
@@ -209,6 +210,16 @@
                 remote(
                     late_part.at[i, lax.rem(core + dc, CORES), lax.rem(x + dx, X)], late_in.at[k],
                     send_sem.at[1], recv_sem.at[0], in_plane(dy, dx, dc),
+                ).start()
+
+    def gather(i):
+        whole_wait(core_in.at[i], core_recv.at[i]).wait_recv()
+        plane_out[i] = part[i, core] + core_in[i]
+        for dx in (2, 1, 3, 0):
+            if Y_ORDER[i] or dx:
+                remote(
+                    plane_out.at[i, lax.rem(x + dx, X)], plane_in.at[(i + 1) % Y * X + dx],
+                    send_sem.at[2], recv_sem.at[1], in_plane(Y_ORDER[i], dx, 0),
                 ).start()
 
     tail = fwd[2 * freqs:].astype(BF16)[:, :6 * freqs]
@@ -245,24 +256,10 @@
                 send_chunk(j)
         elif i > BARRIER_AFTER:
             send_chunk(i)
-
-    def gather(i):
-        whole_wait(core_in.at[i], core_recv.at[i]).wait_recv()
-        plane_out[i] = part[i, core] + core_in[i]
-        for dx in (2, 1, 3, 0):
-            if Y_ORDER[i] or dx:
-                remote(
-                    plane_out.at[i, lax.rem(x + dx, X)], plane_in.at[(i + 1) % Y * X + dx],
-                    send_sem.at[2], recv_sem.at[1], in_plane(Y_ORDER[i], dx, 0),
-                ).start()
-
-    gather(0)
+        if i == Y - 2:
+            gather(0)
+
     gather(1)
-    pl.semaphore_wait(near_sem, 4)
-    for dz in (2, -2):
-        pl.semaphore_signal(far_sem, 1, device_id=in_line(dz), device_id_type=MESH)
-    gather(2)
-
     for copy in inputs[2:7]:
         copy.wait()
     pad[4, :tall, :wide] = wet_int[...].astype(F32)
@@ -281,8 +278,7 @@
     rows_out[0] = pad[:, :REACH, :wide]
     rows_out[1] = pad[:, tall - REACH:tall, :wide]
 
-    gather(Y - 1)
-    pl.semaphore_wait(far_sem, 2)
+    gather(2)
 
     north = (lax.rem(row + n_rows - 1, n_rows), col)
     south = (lax.rem(row + 1, n_rows), col)
@@ -292,10 +288,10 @@
         return remote(source, target, halo_send.at[i], halo_recv.at[i], to)
 
     moves = [
-        (has_n, has_s, halo(rows_out.at[0], rows_in.at[0], 0, north)),
-        (has_s, has_n, halo(rows_out.at[1], rows_in.at[1], 1, south)),
-        (has_w, has_e, halo(strip_out.at[pl.ds(0, 16)], strip_in.at[pl.ds(16, 16)], 2, west)),
-        (has_e, has_w, halo(strip_out.at[pl.ds(16, 16)], strip_in.at[pl.ds(0, 16)], 3, east)),
+        (has_n, has_s, halo(rows_out.at[0], rows_in.at[0], 0, north), True),
+        (has_s, has_n, halo(rows_out.at[1], rows_in.at[1], 1, south), True),
+        (has_w, has_e, halo(strip_out.at[pl.ds(0, 16)], strip_in.at[pl.ds(16, 16)], 2, west), core == 1),
+        (has_e, has_w, halo(strip_out.at[pl.ds(16, 16)], strip_in.at[pl.ds(0, 16)], 3, east), core == 0),
     ]
     for i, (exists, dr, dc) in enumerate(diagonals):
         side = 0 if dr < 0 else 1
@@ -304,11 +300,24 @@
         moves.append((
             exists, diagonals[3 - i][0],
             halo(rows_out.at[side, :, :, cols_at], corner.at[i], 4 + i, to),
+            core == (1 if dc < 0 else 0),
         ))
-    for exists, _, copy in moves:
-        @pl.when(exists)
-        def _(copy=copy):
-            copy.start()
+
+    def send_halos(near_ones):
+        for exists, _, copy, near in moves:
+            if near is True:
+                if near_ones:
+                    pl.when(exists)(copy.start)
+            else:
+                pl.when(exists & (near if near_ones else jnp.logical_not(near)))(copy.start)
+
+    pl.semaphore_wait(near_sem, 4)
+    for dz in (2, -2):
+        pl.semaphore_signal(far_sem, 1, device_id=in_line(dz), device_id_type=MESH)
+    send_halos(True)
+    gather(Y - 1)
+    pl.semaphore_wait(far_sem, 2)
+    send_halos(False)
 
     whole_wait(late_in, recv_sem.at[0]).wait_recv()
     late = late_part[Y - 1, core, x]
@@ -368,55 +377,98 @@
             pl.ds(pl.multiple_of(row * own_steps, own_steps), own_steps)
         ]
 
-    for _, arrives, copy in moves:
-        @pl.when(arrives)
-        def _(copy=copy):
-            copy.wait_recv()
-
-    beside = jnp.concatenate([strip_in[...], jnp.zeros((LANE - 32, tall), F32)], axis=0).T
-    near = lax.broadcasted_iota(jnp.int32, (REACH, LANE), 1) < LANE // 2
+    def arrive(some):
+        for _, arrives, copy, _ in some:
+            @pl.when(arrives)
+            def _(copy=copy):
+                copy.wait_recv()
+
+    arrive(moves[:2])
+    span = wide + LANE
     below, above = pl.ds(tall, REACH), pl.ds(tall + 2 * EDGE - REACH, REACH)
     pad[:, below, :wide] = rows_in[0]
     pad[:, above, :wide] = rows_in[1]
+
+    @pl.when(at_edge)
+    def _():
+        pad[3:5, tall:tall + 1, :wide] = jnp.ones((2, 1, wide), F32)
+
+    def first_step(lanes):
+        face = faces(pad[3, :, lanes], pad[4, :, lanes])
+        for k in range(4):
+            face_buf[k, :, lanes] = face[k]
+        new = step_once(*(pad[k, :, lanes] for k in range(5)), face)
+        for k in range(3):
+            mid[k, :, lanes] = new[k]
+
+    def second_step(lanes):
+        face = [face_buf[k, :, lanes] for k in range(4)]
+        state = [mid[k, :, lanes] for k in range(3)]
+        return step_once(*state, pad[3, :, lanes], pad[4, :, lanes], face)
+
+    def place_sides(k, rows, sides):
+        at = lax.broadcasted_iota(jnp.int32, sides.shape, 1)
+        first, last = pl.ds(0, LANE), pl.ds(wide - LANE, LANE)
+        out_buf[k, rows, first] = jnp.where(
+            at < REACH, pltpu.roll(sides, LANE - SHIFT, 1), out_buf[k, rows, first]
+        )
+        out_buf[k, rows, last] = jnp.where(
+            at >= LANE - REACH, pltpu.roll(sides, SHIFT, 1), out_buf[k, rows, last]
+        )
+
+    body, border = pl.ds(0, wide), pl.ds(wide, LANE)
+    first_step(body)
+    new = second_step(body)
+    for k in range(3):
+        out_buf[k] = new[k][:tall]
+    left = lax.broadcasted_iota(jnp.int32, (tall + 2 * EDGE, LANE), 1) < LANE // 2
     for k in range(5):
-        pad[k, :tall, wide:] = jnp.where(
-            lane < LANE // 2,
-            pltpu.roll(beside, LANE - 16 - 2 * k, 1),
-            pltpu.roll(beside, LANE - 2 - 2 * k, 1),
-        )
-        pad[k, below, wide:] = jnp.where(near, corner[0, k], corner[1, k])
-        pad[k, above, wide:] = jnp.where(near, corner[2, k], corner[3, k])
+        pad[k, :, border] = jnp.where(
+            left,
+            pltpu.roll(pad[k, :, wide - LANE:wide], LANE - SHIFT, 1),
+            pltpu.roll(pad[k, :, :LANE], SHIFT, 1),
+        )
+
+    arrive(moves[2:])
+    beside = jnp.concatenate([strip_in[...], jnp.zeros((LANE - 32, tall), F32)], axis=0).T
+    edge_at = LANE // 2 - REACH
+
+    def lay(k, rows, from_west, from_east):
+        at = lax.broadcasted_iota(jnp.int32, from_west.shape, 1)
+        value = jnp.where(at < LANE // 2, from_east, from_west)
+        pad[k, rows, border] = jnp.where(
+            (at >= edge_at) & (at < edge_at + 2 * REACH), value, pad[k, rows, border]
+        )
+
+    for k in range(5):
+        lay(
+            k, pl.ds(0, tall), pltpu.roll(beside, LANE // 2 - 2 * k, 1),
+            pltpu.roll(beside, edge_at - 16 - 2 * k, 1),
+        )
+        for i, rows in ((0, below), (2, above)):
+            lay(
+                k, rows, pltpu.roll(corner[i + 1, k], SHIFT, 1),
+                pltpu.roll(corner[i, k], edge_at, 1),
+            )
 
     @pl.when(at_edge)
     def _():
-        pad[3:5, tall:tall + 1, :] = jnp.ones((2, 1, wide + LANE), F32)
-
-    def first_step():
-        face = faces(pad[3], pad[4])
-        for k in range(4):
-            face_buf[k] = face[k]
-        new = step_once(pad[0], pad[1], pad[2], pad[3], pad[4], face)
-        for k in range(3):
-            mid[k] = new[k]
-
-    def second_step():
-        face = [face_buf[k] for k in range(4)]
-        new = step_once(mid[0], mid[1], mid[2], pad[3], pad[4], face)
-        for k in range(3):
-            out_buf[k] = new[k][:tall, :wide]
-
-    first_step()
+        pad[3:5, tall:tall + 1, wide:] = jnp.ones((2, 1, LANE), F32)
+
+    first_step(border)
+    new = second_step(border)
+    for k in range(3):
+        place_sides(k, pl.ds(0, tall), new[k][:tall])
 
     inputs[8].wait()
-    span = wide + LANE
 
     @pl.when(at_edge)
     def _():
         place = lax.broadcasted_iota(jnp.int32, (span, obs), 0)
-        place = jnp.where(place >= wide + LANE // 2, place - span, place) + col * wide
+        place = col * wide + place - jnp.where(
+            place >= wide + LANE // 2, wide + SHIFT, jnp.where(place >= wide, SHIFT - REACH - REACH, 0)
+        )
         chosen_buf[...] = jnp.where(place == cells[...], 1.0, 0.0).astype(BF16)
-
-    second_step()
 
     @pl.when(home)
     def _():
@@ -449,24 +501,28 @@
         picked = picked[0:2] + picked[2:4] + picked[4:6]
         base = tall - 2 * EDGE
         part_rows = pl.ds(base, 3 * EDGE)
-        at_ghost = lax.broadcasted_iota(jnp.int32, (3 * EDGE, span), 0) == 2 * EDGE
-        ghosts = [
-            jnp.broadcast_to(picked[k:k + 1], (3 * EDGE, span)) for k in range(2)
-        ]
-        wet, speed_sq = pad[4, part_rows], pad[3, part_rows]
-        face = [face_buf[k, part_rows] for k in range(4)]
-        surf = jnp.where(at_ghost, ghosts[0], pad[0, part_rows])
-        surf, qx, qy = step_once(
-            surf, pad[1, part_rows], pad[2, part_rows], speed_sq, wet, face
-        )
-        surf = jnp.where(at_ghost, ghosts[1], surf)
-        qx = jnp.where(at_ghost, 0.0, qx)
-        qy = jnp.where(at_ghost, 0.0, qy)
-        new = step_once(surf, qx, qy, speed_sq, wet, face)
-        for k in range(3):
-            out_buf[k, tall - EDGE:] = new[k][EDGE:2 * EDGE, :wide]
-
-    for exists, _, copy in moves:
+        for lanes in (body, border):
+            width = lanes.size
+            picks = picked[:, lanes.start:lanes.start + width]
+            at_ghost = lax.broadcasted_iota(jnp.int32, (3 * EDGE, width), 0) == 2 * EDGE
+            ghosts = [jnp.broadcast_to(picks[k:k + 1], (3 * EDGE, width)) for k in range(2)]
+            speed_sq, wet = pad[3, part_rows, lanes], pad[4, part_rows, lanes]
+            face = [face_buf[k, part_rows, lanes] for k in range(4)]
+            surf = jnp.where(at_ghost, ghosts[0], pad[0, part_rows, lanes])
+            surf, qx, qy = step_once(
+                surf, pad[1, part_rows, lanes], pad[2, part_rows, lanes], speed_sq, wet, face
+            )
+            surf = jnp.where(at_ghost, ghosts[1], surf)
+            qx = jnp.where(at_ghost, 0.0, qx)
+            qy = jnp.where(at_ghost, 0.0, qy)
+            new = step_once(surf, qx, qy, speed_sq, wet, face)
+            for k in range(3):
+                if width == wide:
+                    out_buf[k, tall - EDGE:] = new[k][EDGE:2 * EDGE]
+                else:
+                    place_sides(k, pl.ds(tall - EDGE, EDGE), new[k][EDGE:2 * EDGE])
+
+    for exists, _, copy, _ in moves:
         @pl.when(exists)
         def _(copy=copy):
             copy.wait_send()

time: 25.5 us -> 24.3 us (0.953)
  Pallas kernels: 24.7 us -> 23.5 us
    pallas_call x1, Pallas kernels: 23.8 us -> 22.6 us  [on_device(): pl.pallas_call(functools.partial(kernel, n_rows, n_cols), out_shape=(pltp...]
where the time goes in v3:
time: 24.3 us; the launch traced here: 24.2 us
  Pallas kernels  23.5 us (97%)
  between operations  0.64 us (3%)
    pallas_call x1, Pallas kernels, on_device(): pl.pallas_call(functools.partial(kernel, n_rows, n_cols), out_shape=(pltp...  22.6 us
    pallas_call x1, Pallas kernels, on_device(): pl.pallas_call(write_out, out_shape=(jax.ShapeDtypeStruct((own_steps, poi...  0.92 us

profile of v3, /device:TPU:1, one launch (start us, length us, event | category | flops | bytes accessed | tf_op | source)
XLA Modules:
  0.0 24.2 jit_solution(11566686282846849275)
XLA Ops:
  0.6 22.6 %shard_map.129 = (f32[8,256]{1,0:T(8,128)S(1)}, f32[3,256,256]{2,1,0:T(8,128)S(1)}) custom-call(bf16[2,16,32,4096]{3,2,1,0:T(8,128)(2,1)} %kern_hbm.1, f32[32,128]{1,0:T(8,128)} %bitcast.2, f32[256,256]{1,0:T(8,128)} %sq_hbm.1, s32[256,256]{1,0:T(8,128)} %wet_hbm.1, s32[1,4096]{1,0:T(1,128)} %bitcast.3, f32[256,256]{1,0:T(8,128)} %surf_hbm.1, ...), custom_call_target="tpu_custom_call" | custom-call | tf_op jit(solution)/shard_map/pallas_call | solution.py:573
  23.3 0.9 %shard_map.130 = (f32[8,256]{1,0:T(8,128)}, f32[256,256]{1,0:T(8,128)}, f32[256,256]{1,0:T(8,128)}, f32[256,256]{1,0:T(8,128)}) custom-call(f32[8,256]{1,0:T(8,128)S(1)} %get-tuple-element.6.series, f32[3,256,256]{2,1,0:T(8,128)S(1)} %get-tuple-element.7.fields), custom_call_target="tpu_custom_call" | custom-call | tf_op jit(solution)/shard_map/pallas_call | solution.py:625

commit v4 on v3

--- a/solution.py
+++ b/solution.py
@@ -83,8 +83,8 @@
     series_buf, out_buf,
     kern, coef, fwd, inv, cells, pad, wet_int, corner, rows_out, rows_in, strip_out, strip_in,
     part, core_in, plane_out, plane_in, spec_buf, whole_buf, whole_in,
-    late_part, late_in, late_out, edge_in, face_buf, mid, chosen_buf,
-    local_sem, kern_sem, core_recv, halo_send, halo_recv, send_sem, recv_sem, near_sem, far_sem,
+    late_part, late_in, late_out, edge_in, both_cores, face_buf, mid, chosen_buf,
+    local_sem, kern_sem, core_recv, halo_send, halo_recv, recv_sem, near_sem, far_sem,
 ):
     row = lax.axis_index("rows")
     col = lax.axis_index("cols")
@@ -106,25 +106,22 @@
         pltpu.make_async_copy(coef_hbm, coef, local_sem.at[0]),
         pltpu.make_async_copy(fwd_hbm.at[row], fwd, local_sem.at[1]),
         pltpu.make_async_copy(surf_hbm, pad.at[0, :tall, :wide], local_sem.at[3]),
-        pltpu.make_async_copy(qx_hbm, pad.at[1, :tall, :wide], local_sem.at[4]),
-        pltpu.make_async_copy(qy_hbm, pad.at[2, :tall, :wide], local_sem.at[5]),
-        pltpu.make_async_copy(sq_hbm, pad.at[3, :tall, :wide], local_sem.at[6]),
-        pltpu.make_async_copy(wet_hbm, wet_int, local_sem.at[7]),
+        pltpu.make_async_copy(qx_hbm, pad.at[1, :tall, :wide], local_sem.at[3]),
+        pltpu.make_async_copy(qy_hbm, pad.at[2, :tall, :wide], local_sem.at[3]),
+        pltpu.make_async_copy(sq_hbm, pad.at[3, :tall, :wide], local_sem.at[3]),
+        pltpu.make_async_copy(wet_hbm, wet_int, local_sem.at[3]),
         pltpu.make_async_copy(inv_hbm.at[z_low], inv, local_sem.at[2]),
-        pltpu.make_async_copy(cell_hbm, cells, local_sem.at[8]),
+        pltpu.make_async_copy(cell_hbm, cells, local_sem.at[4]),
     ]
     for copy in inputs[:2]:
         copy.start()
     chunks = []
     for i, dy in enumerate(Y_ORDER):
         at = pl.multiple_of(lax.rem(y + dy, Y) * per_y, per_y)
-        for p in range(2):
-            copy = pltpu.make_async_copy(
-                kern_hbm.at[p, :, :, pl.ds(at, per_y)], kern.at[i, p], kern_sem.at[i, p]
-            )
-            chunks.append(copy)
-    for copy in chunks[:2]:
-        copy.start()
+        chunks.append(pltpu.make_async_copy(
+            kern_hbm.at[:, :, :, pl.ds(at, per_y)], kern.at[i], kern_sem.at[i]
+        ))
+    chunks[0].start()
     pad[:, tall:] = jnp.zeros((5, 2 * EDGE, wide + LANE), F32)
     rows_in[...] = jnp.zeros(rows_in.shape, F32)
     strip_in[...] = jnp.zeros(strip_in.shape, F32)
@@ -160,11 +157,10 @@
 
     for dz in (2, -2, 1, -1):
         greet(in_line(dz))
-    for copy in chunks[2:4]:
-        copy.start()
+    chunks[1].start()
     for dy, dx, dc in plane:
         greet(in_plane(dy, dx, dc))
-    for copy in chunks[4:]:
+    for copy in chunks[2:]:
         copy.start()
     for copy in inputs[2:]:
         copy.start()
@@ -203,13 +199,13 @@
 
     def send_chunk(i):
         remote(
-            part.at[i, 1 - core], core_in.at[i], send_sem.at[0], core_recv.at[i], partner_core
+            part.at[i, 1 - core], core_in.at[i], local_sem.at[0], core_recv.at[i], partner_core
         ).start()
         for k, (dy, dx, dc) in enumerate(plane):
             if dy == Y_ORDER[i]:
                 remote(
                     late_part.at[i, lax.rem(core + dc, CORES), lax.rem(x + dx, X)], late_in.at[k],
-                    send_sem.at[1], recv_sem.at[0], in_plane(dy, dx, dc),
+                    local_sem.at[1], recv_sem.at[0], in_plane(dy, dx, dc),
                 ).start()
 
     def gather(i):
@@ -219,13 +215,12 @@
             if Y_ORDER[i] or dx:
                 remote(
                     plane_out.at[i, lax.rem(x + dx, X)], plane_in.at[(i + 1) % Y * X + dx],
-                    send_sem.at[2], recv_sem.at[1], in_plane(Y_ORDER[i], dx, 0),
+                    kern_sem.at[0], recv_sem.at[1], in_plane(Y_ORDER[i], dx, 0),
                 ).start()
 
     tail = fwd[2 * freqs:].astype(BF16)[:, :6 * freqs]
     for i in range(Y):
-        chunks[2 * i].wait()
-        chunks[2 * i + 1].wait()
+        chunks[i].wait()
         totals = []
         for g in range(groups):
             total = None
@@ -260,8 +255,8 @@
             gather(0)
 
     gather(1)
-    for copy in inputs[2:7]:
-        copy.wait()
+    fields = pad.at[:, :tall, :wide]
+    pltpu.make_async_copy(fields, fields, local_sem.at[3]).wait()
     pad[4, :tall, :wide] = wet_int[...].astype(F32)
     lane = lax.broadcasted_iota(jnp.int32, (tall, LANE), 1)
     packed = jnp.zeros((tall, LANE), F32)
@@ -324,13 +319,15 @@
     for k in range(len(plane)):
         late = late + late_in[k]
     late_out[...] = late
-    block = ((y * Z_HIGH + x // 2) * CORES + core) * 2 + lax.rem(x, 2)
-    blocks = obs // LANE
-    for k in range(n_cols):
+    slot = z * (Y * X) + y * X + x
+    slots = depth * Y * X
+    edges = Y * Z_HIGH
+    own_edge = y * Z_HIGH + z_high
+    for k in range(edges):
         def _(k=k):
+            to = lax.rem(own_edge + k, edges) * CORES + core
             remote(
-                late_out, edge_in.at[z * blocks + block], send_sem.at[3], recv_sem.at[2],
-                (n_rows - 1, lax.rem(col + k, n_cols)),
+                late_out, edge_in.at[slot], kern_sem.at[1], recv_sem.at[2], (n_rows - 1, to)
             ).start()
         if k:
             _()
@@ -339,7 +336,7 @@
 
     @pl.when(at_edge)
     def _():
-        edge_in[z * blocks + block] = late
+        edge_in[slot] = late
 
     others = plane_in.at[pl.ds(1, X * Y - 1)]
     whole_wait(others, recv_sem.at[1]).wait_recv()
@@ -357,19 +354,15 @@
     whole_buf[...] = whole
     z_base = x // 2 * Z_LOW
     own_half = lax.rem(x, 2) * depth
-    for k in range(n_rows):
-        def _(k=k):
-            to = lax.rem(row + k, n_rows)
+    for to in range(n_rows):
+        @pl.when(jnp.logical_not(home & (row == to)))
+        def _(to=to):
             z_to = z_base + to // X
             remote(
-                whole_buf.at[pl.ds(pl.multiple_of(to * own_steps, own_steps), own_steps)],
+                whole_buf.at[pl.ds(to * own_steps, own_steps)],
                 whole_in.at[own_half + lax.rem(z_to - z + depth, depth)],
-                send_sem.at[4], recv_sem.at[3], device(lax.rem(to, X), y, z_to, core),
+                kern_sem.at[2], recv_sem.at[3], device(to % X, y, z_to, core),
             ).start()
-        if k:
-            _()
-        else:
-            pl.when(jnp.logical_not(home))(_)
 
     @pl.when(home)
     def _():
@@ -469,6 +462,14 @@
             place >= wide + LANE // 2, wide + SHIFT, jnp.where(place >= wide, SHIFT - REACH - REACH, 0)
         )
         chosen_buf[...] = jnp.where(place == cells[...], 1.0, 0.0).astype(BF16)
+        whole_wait(edge_in.at[pl.ds(0, slots - 1)], recv_sem.at[2]).wait_recv()
+        total = edge_in[pl.ds(0, Y * X)]
+        for k in range(1, depth):
+            total = total + edge_in[pl.ds(k * Y * X, Y * X)]
+        both_cores[core] = total
+        remote(
+            both_cores.at[core], both_cores.at[core], kern_sem.at[3], recv_sem.at[4], partner_core
+        ).start()
 
     @pl.when(home)
     def _():
@@ -486,11 +487,11 @@
 
     @pl.when(at_edge)
     def _():
-        whole_wait(edge_in.at[pl.ds(0, depth * blocks - 1)], recv_sem.at[2]).wait_recv()
-        total = edge_in[pl.ds(0, blocks)]
-        for k in range(1, depth):
-            total = total + edge_in[pl.ds(k * blocks, blocks)]
-        latest = jnp.concatenate([total[b] for b in range(blocks)], axis=1)
+        whole_wait(both_cores.at[0], recv_sem.at[4]).wait_recv()
+        latest = jnp.concatenate([
+            both_cores[c, y_at * X + h * 2 + half]
+            for y_at in range(Y) for h in range(Z_HIGH) for c in range(CORES) for half in range(2)
+        ], axis=1)
         high, rest = split(latest)
         middle, rest = split(rest)
         parts = jnp.concatenate([high.astype(F32), middle.astype(F32), rest, rest], axis=0)
@@ -527,26 +528,27 @@
         def _(copy=copy):
             copy.wait_send()
     for ref, sem in (
-        (core_in, send_sem.at[0]), (late_in, send_sem.at[1]),
-        (others, send_sem.at[2]),
+        (core_in, local_sem.at[0]), (late_in, local_sem.at[1]),
+        (others, kern_sem.at[0]),
     ):
         whole_wait(ref, sem).wait_send()
 
     @pl.when(at_edge)
     def _():
-        whole_wait(edge_in.at[pl.ds(0, n_cols - 1)], send_sem.at[3]).wait_send()
+        whole_wait(edge_in.at[pl.ds(0, edges - 1)], kern_sem.at[1]).wait_send()
+        whole_wait(both_cores.at[0], kern_sem.at[3]).wait_send()
 
     @pl.when(jnp.logical_not(at_edge))
     def _():
-        whole_wait(edge_in.at[pl.ds(0, n_cols)], send_sem.at[3]).wait_send()
+        whole_wait(edge_in.at[pl.ds(0, edges)], kern_sem.at[1]).wait_send()
 
     @pl.when(home)
     def _():
-        whole_wait(whole_in.at[pl.ds(0, 2 * depth - 1)], send_sem.at[4]).wait_send()
+        whole_wait(whole_in.at[pl.ds(0, 2 * depth - 1)], kern_sem.at[2]).wait_send()
 
     @pl.when(jnp.logical_not(home))
     def _():
-        whole_wait(whole_in, send_sem.at[4]).wait_send()
+        whole_wait(whole_in, kern_sem.at[2]).wait_send()
 
 
 def write_out(series, fields, series_hbm, surf_hbm, qx_hbm, qy_hbm, sems):
@@ -601,17 +603,17 @@
             pltpu.VMEM((Y, CORES, X, 2, LANE), F32),
             pltpu.VMEM((Y * X * CORES - 1, 2, LANE), F32),
             pltpu.VMEM((2, LANE), F32),
-            pltpu.VMEM((Z_LOW * Z_HIGH * (obs // LANE), 2, LANE), F32),
+            pltpu.VMEM((Z_LOW * Z_HIGH * Y * X, 2, LANE), F32),
+            pltpu.VMEM((CORES, Y * X, 2, LANE), F32),
             pltpu.VMEM((4, tall + 2 * EDGE, span), F32),
             pltpu.VMEM((3, tall + 2 * EDGE, span), F32),
             pltpu.VMEM((span, obs), BF16),
-            dma((9,)),
-            dma((Y, 2)),
+            dma((5,)),
+            dma((Y,)),
             dma((Y,)),
             dma((8,)),
             dma((8,)),
             dma((5,)),
-            dma((4,)),
             pltpu.SemaphoreType.REGULAR,
             pltpu.SemaphoreType.REGULAR,
         ],

time: 24.3 us -> 24.2 us (level)
  Pallas kernels: 23.5 us -> 23.2 us
    pallas_call x1, Pallas kernels: 22.6 us -> 22.3 us  [on_device(): pl.pallas_call(functools.partial(kernel, n_rows, n_cols), out_shape=(pltp...]
where the time goes in v4:
time: 24.2 us; the launch traced here: 23.8 us
  Pallas kernels  23.2 us (96%)
  between operations  0.64 us (3%)
    pallas_call x1, Pallas kernels, on_device(): pl.pallas_call(functools.partial(kernel, n_rows, n_cols), out_shape=(pltp...  22.3 us
    pallas_call x1, Pallas kernels, on_device(): pl.pallas_call(write_out, out_shape=(jax.ShapeDtypeStruct((own_steps, poi...  0.92 us

profile of v4, /device:TPU:1, one launch (start us, length us, event | category | flops | bytes accessed | tf_op | source)
XLA Modules:
  0.0 23.8 jit_solution(9327199680998183137)
XLA Ops:
  0.6 22.3 %shard_map.129 = (f32[8,256]{1,0:T(8,128)S(1)}, f32[3,256,256]{2,1,0:T(8,128)S(1)}) custom-call(bf16[2,16,32,4096]{3,2,1,0:T(8,128)(2,1)} %kern_hbm.1, f32[32,128]{1,0:T(8,128)} %bitcast.2, f32[256,256]{1,0:T(8,128)} %sq_hbm.1, s32[256,256]{1,0:T(8,128)} %wet_hbm.1, s32[1,4096]{1,0:T(1,128)} %bitcast.3, f32[256,256]{1,0:T(8,128)} %surf_hbm.1, ...), custom_call_target="tpu_custom_call" | custom-call | tf_op jit(solution)/shard_map/pallas_call | solution.py:575
  22.9 0.9 %shard_map.130 = (f32[8,256]{1,0:T(8,128)}, f32[256,256]{1,0:T(8,128)}, f32[256,256]{1,0:T(8,128)}, f32[256,256]{1,0:T(8,128)}) custom-call(f32[8,256]{1,0:T(8,128)S(1)} %get-tuple-element.6.series, f32[3,256,256]{2,1,0:T(8,128)S(1)} %get-tuple-element.7.fields), custom_call_target="tpu_custom_call" | custom-call | tf_op jit(solution)/shard_map/pallas_call | solution.py:627

commit v5 on v4

--- a/solution.py
+++ b/solution.py
@@ -15,7 +15,6 @@
 REACH = 2
 SHIFT = LANE // 2 + REACH
 X, Y, Z_LOW, Z_HIGH, CORES = 4, 4, 4, 2, 2
-Y_ORDER = (2, 1, 3, 0)
 BARRIER_AFTER = 1
 EDGE = 8
 F32 = jnp.float32
@@ -116,8 +115,16 @@
     for copy in inputs[:2]:
         copy.start()
     chunks = []
-    for i, dy in enumerate(Y_ORDER):
-        at = pl.multiple_of(lax.rem(y + dy, Y) * per_y, per_y)
+    first_y = y == 0
+    y_to = [
+        0,
+        jnp.where(first_y, 2, jnp.where(y == 1, 3, 1)),
+        jnp.where(first_y, 1, jnp.where(y == 2, 3, 2)),
+        jnp.where(first_y, 3, y),
+    ]
+    own_turn = jnp.where(first_y, 0, Y - 1)
+    for i in range(Y):
+        at = pl.multiple_of(y_to[i] * per_y, per_y)
         chunks.append(pltpu.make_async_copy(
             kern_hbm.at[:, :, :, pl.ds(at, per_y)], kern.at[i], kern_sem.at[i]
         ))
@@ -201,22 +208,36 @@
         remote(
             part.at[i, 1 - core], core_in.at[i], local_sem.at[0], core_recv.at[i], partner_core
         ).start()
-        for k, (dy, dx, dc) in enumerate(plane):
-            if dy == Y_ORDER[i]:
-                remote(
-                    late_part.at[i, lax.rem(core + dc, CORES), lax.rem(x + dx, X)], late_in.at[k],
-                    local_sem.at[1], recv_sem.at[0], in_plane(dy, dx, dc),
-                ).start()
+        ahead = lax.rem(y_to[i] - y + Y, Y) * X
+        for dx in range(X):
+            for dc in range(CORES):
+                def send(dx=dx, dc=dc):
+                    x_to, core_to = lax.rem(x + dx, X), lax.rem(core + dc, CORES)
+                    remote(
+                        late_part.at[i, core_to, x_to],
+                        late_in.at[lax.max((ahead + dx) * CORES + dc - 1, 0)],
+                        local_sem.at[1], recv_sem.at[0], device(x_to, y_to[i], z, core_to),
+                    ).start()
+                if dx or dc:
+                    send()
+                else:
+                    pl.when(own_turn != i)(send)
 
     def gather(i):
         whole_wait(core_in.at[i], core_recv.at[i]).wait_recv()
         plane_out[i] = part[i, core] + core_in[i]
+        ahead = lax.rem(y_to[i] - y + Y, Y) * X
         for dx in (2, 1, 3, 0):
-            if Y_ORDER[i] or dx:
+            def send(dx=dx):
+                x_to = lax.rem(x + dx, X)
                 remote(
-                    plane_out.at[i, lax.rem(x + dx, X)], plane_in.at[(i + 1) % Y * X + dx],
-                    kern_sem.at[0], recv_sem.at[1], in_plane(Y_ORDER[i], dx, 0),
+                    plane_out.at[i, x_to], plane_in.at[ahead + dx],
+                    kern_sem.at[0], recv_sem.at[1], device(x_to, y_to[i], z, core),
                 ).start()
+            if dx:
+                send()
+            else:
+                pl.when(own_turn != i)(send)
 
     tail = fwd[2 * freqs:].astype(BF16)[:, :6 * freqs]
     for i in range(Y):
@@ -315,7 +336,7 @@
     send_halos(False)
 
     whole_wait(late_in, recv_sem.at[0]).wait_recv()
-    late = late_part[Y - 1, core, x]
+    late = late_part[own_turn, core, x]
     for k in range(len(plane)):
         late = late + late_in[k]
     late_out[...] = late
@@ -341,7 +362,7 @@
     others = plane_in.at[pl.ds(1, X * Y - 1)]
     whole_wait(others, recv_sem.at[1]).wait_recv()
     for dx in range(X):
-        value = plane_out[Y - 1, x] if dx == 0 else plane_in[dx]
+        value = plane_out[own_turn, x] if dx == 0 else plane_in[dx]
         for i in range(Y - 1):
             value = value + plane_in[(i + 1) * X + dx]
         spec_buf[lax.rem(x + X - dx, X)] = value

time: 24.2 us -> 23.8 us (0.983)
  Pallas kernels: 23.2 us -> 22.8 us
    pallas_call x1, Pallas kernels: 22.3 us -> 21.9 us  [on_device(): pl.pallas_call(functools.partial(kernel, n_rows, n_cols), out_shape=(pltp...]
where the time goes in v5:
time: 23.8 us; the launch traced here: 23.4 us
  Pallas kernels  22.8 us (96%)
  between operations  0.64 us (3%)
    pallas_call x1, Pallas kernels, on_device(): pl.pallas_call(functools.partial(kernel, n_rows, n_cols), out_shape=(pltp...  21.9 us
    pallas_call x1, Pallas kernels, on_device(): pl.pallas_call(write_out, out_shape=(jax.ShapeDtypeStruct((own_steps, poi...  0.92 us

profile of v5, /device:TPU:1, one launch (start us, length us, event | category | flops | bytes accessed | tf_op | source)
XLA Modules:
  0.0 23.4 jit_solution(12893103147630533261)
XLA Ops:
  0.6 21.9 %shard_map.129 = (f32[8,256]{1,0:T(8,128)S(1)}, f32[3,256,256]{2,1,0:T(8,128)S(1)}) custom-call(bf16[2,16,32,4096]{3,2,1,0:T(8,128)(2,1)} %kern_hbm.1, f32[32,128]{1,0:T(8,128)} %bitcast.2, f32[256,256]{1,0:T(8,128)} %sq_hbm.1, s32[256,256]{1,0:T(8,128)} %wet_hbm.1, s32[1,4096]{1,0:T(1,128)} %bitcast.3, f32[256,256]{1,0:T(8,128)} %surf_hbm.1, ...), custom_call_target="tpu_custom_call" | custom-call | tf_op jit(solution)/shard_map/pallas_call | solution.py:596
  22.5 0.9 %shard_map.130 = (f32[8,256]{1,0:T(8,128)}, f32[256,256]{1,0:T(8,128)}, f32[256,256]{1,0:T(8,128)}, f32[256,256]{1,0:T(8,128)}) custom-call(f32[8,256]{1,0:T(8,128)S(1)} %get-tuple-element.6.series, f32[3,256,256]{2,1,0:T(8,128)S(1)} %get-tuple-element.7.fields), custom_call_target="tpu_custom_call" | custom-call | tf_op jit(solution)/shard_map/pallas_call | solution.py:648
